TPU v7x, 16 devices: a whole 2x2x2 slice. The times are simulated.
16 devices in a mesh: dp: 2 (over z), ep: 8 (over y, x, core).
Axes of the slice: x: 2, y: 2, z: 2, core: 2. Of those that a mesh axis runs over, the one named last changes fastest.
Arguments:
- h0: bfloat16 [16, 256, 2048], P(('dp', 'ep')), parts along dimension 0
- idx: int32 [16, 256, 8], P(('dp', 'ep')), parts along dimension 0
- slot: int32 [16, 256, 8], P(('dp', 'ep')), parts along dimension 0
- norm_attn: bfloat16 [2048], replicated
- wq: bfloat16 [2048, 2048], replicated
- wk: bfloat16 [2048, 2048], replicated
- wv: bfloat16 [2048, 2048], replicated
- wo: bfloat16 [2048, 2048], replicated
- norm_ffn: bfloat16 [2048], replicated
- w1: bfloat16 [2048, 8192], replicated
- w3: bfloat16 [2048, 8192], replicated
- w2: bfloat16 [8192, 2048], replicated
- norm_moe: bfloat16 [2048], replicated
- wr: bfloat16 [2048, 64], replicated
- ue1: bfloat16 [64, 2048, 1024], P('ep')
- ue3: bfloat16 [64, 2048, 1024], P('ep')
- ue2: bfloat16 [64, 1024, 2048], P('ep')
Outputs:
- output: bfloat16 [16, 256, 2048], P(('dp', 'ep')), parts along dimension 0
There are 2 independent parts. A program takes and returns all parts, laid end to end along the dimension named above; an argument that names none is the same for every part.
All inputs are finite; a program needn't handle non-finite values.
Results may differ from a plain program's by a relative error of at most 0.0105677.
Values are sent between devices in bfloat16 or wider.
A program may use at most 1 GiB of HBM per device.

v0:
```python
import jax
import jax.numpy as jnp
from jax import lax
from jax.sharding import PartitionSpec as P

HEAD = 128
EPS = 1e-6
ROPE_BASE = 10000.0


def _rms(x, w):
    xf = x.astype(jnp.float32)
    r = lax.rsqrt(jnp.mean(xf * xf, axis=-1, keepdims=True) + EPS)
    return (xf * r * w.astype(jnp.float32)).astype(jnp.bfloat16)


def _rope(x, cos, sin):
    h = HEAD // 2
    x1, x2 = x[..., :h], x[..., h:]
    return jnp.concatenate([x1 * cos - x2 * sin, x2 * cos + x1 * sin], axis=-1)


def _dense(h0, na, wq, wk, wv, wo, nf, w1, w3, w2):
    f32, bf = jnp.float32, jnp.bfloat16
    b, s, d = h0.shape
    nh = wq.shape[1] // HEAD
    nkvv = wk.shape[1] // HEAD
    pos = jnp.arange(s).astype(f32)
    inv = ROPE_BASE ** (-2.0 * jnp.arange(HEAD // 2).astype(f32) / HEAD)
    ang = pos[:, None] * inv[None, :]
    cos, sin = jnp.cos(ang)[:, None, :], jnp.sin(ang)[:, None, :]
    x = _rms(h0, na).reshape(b * s, d)
    q = _rope(jnp.dot(x, wq, preferred_element_type=f32).reshape(b, s, nh, HEAD), cos, sin).astype(bf)
    k = _rope(jnp.dot(x, wk, preferred_element_type=f32).reshape(b, s, nkvv, HEAD), cos, sin).astype(bf)
    v = jnp.dot(x, wv, preferred_element_type=f32).astype(bf).reshape(b, s, nkvv, HEAD)
    q = q.reshape(b, s, nkvv, nh // nkvv, HEAD)
    sc = jnp.einsum('bqgrd,bkgd->bgrqk', q, k, preferred_element_type=f32) * HEAD ** -0.5
    causal = jnp.arange(s)[:, None] >= jnp.arange(s)[None, :]
    sc = jnp.where(causal, sc, -jnp.inf)
    p = jax.nn.softmax(sc, axis=-1).astype(bf)
    o = jnp.einsum('bgrqk,bkgd->bqgrd', p, v, preferred_element_type=f32).astype(bf).reshape(b * s, nh * HEAD)
    a = (h0.reshape(b * s, d).astype(f32) + jnp.dot(o, wo, preferred_element_type=f32)).astype(bf)
    z = _rms(a, nf)
    hid = (jax.nn.silu(jnp.dot(z, w1, preferred_element_type=f32)) * jnp.dot(z, w3, preferred_element_type=f32)).astype(bf)
    return a.astype(f32) + jnp.dot(hid, w2, preferred_element_type=f32)


def _route(h0, nm, wr, idx):
    d = h0.shape[-1]
    k = idx.shape[-1]
    u = _rms(h0, nm).reshape(-1, d)
    logits = jnp.dot(u, wr, preferred_element_type=jnp.float32)
    g = jax.nn.softmax(jnp.take_along_axis(logits, idx.reshape(-1, k), axis=1), axis=-1)
    return u, g


def _experts(x, ue1, ue3, ue2):
    f32 = jnp.float32
    h1 = jnp.einsum('ecd,edf->ecf', x, ue1, preferred_element_type=f32)
    h3 = jnp.einsum('ecd,edf->ecf', x, ue3, preferred_element_type=f32)
    hid = (jax.nn.silu(h1) * h3).astype(jnp.bfloat16)
    return jnp.einsum('ecf,efd->ecd', hid, ue2, preferred_element_type=f32).astype(jnp.bfloat16)


def solution(mesh):
    G = mesh.shape['ep']

    def local(h0, idx, slot, na, wq, wk, wv, wo, nf, w1, w3, w2, nm, wr, ue1, ue3, ue2):
        f32 = jnp.float32
        b, s, d = h0.shape
        t = b * s
        k = idx.shape[-1]
        el = ue1.shape[0]
        e = el * G
        cap = 2 * t * k // e
        u, g = _route(h0, nm, wr, idx)
        ix = idx.reshape(t, k)
        sl = slot.reshape(t, k)
        rows = jnp.broadcast_to(jnp.arange(t, dtype=jnp.int32)[:, None], (t, k))
        tok = jnp.full((e, cap), t, jnp.int32).at[ix, sl].set(rows)
        send = jnp.take(u, tok, axis=0, mode='fill', fill_value=0)
        recv = lax.all_to_all(send, 'ep', 0, 0, tiled=True)
        x = recv.reshape(G, el, cap, d).transpose(1, 0, 2, 3).reshape(el, G * cap, d)
        y = _experts(x, ue1, ue3, ue2)
        y = y.reshape(el, G, cap, d).transpose(1, 0, 2, 3).reshape(e, cap, d)
        back = lax.all_to_all(y, 'ep', 0, 0, tiled=True)
        yg = back[ix, sl]
        m = jnp.sum(g[..., None] * yg.astype(f32), axis=1)
        dense = _dense(h0, na, wq, wk, wv, wo, nf, w1, w3, w2)
        return (dense + m).astype(jnp.bfloat16).reshape(b, s, d)

    rows_spec = P(('dp', 'ep'))
    in_specs = (rows_spec,) * 3 + (P(),) * 11 + (P('ep'),) * 3
    return jax.shard_map(local, mesh=mesh, in_specs=in_specs, out_specs=rows_spec, check_vma=False)
```

profile of v0, /device:TPU:0, one launch (start us, length us, event | category | flops | bytes accessed | tf_op | source)
XLA Modules:
  0.0 612.0 jit_solution(4588174520515256129)
XLA Ops:
  0.0 1.4 shift-left_or_fusion
  1.4 0.7 multiply_reduce_fusion
  2.5 8.1 %scatter_custom_fusion = s32[4096]{0:T(1024)S(1)} fusion(s32[2048]{0:T(1024)S(1)} %reshape.352, s32[2048]{0:T(1024)S(1)} %reshape.354, s32[]{:T(128)} %constant.59.clone.1), kind=kCustom, calls=%fused_computation.89 | custom fusion | bytes 16388
  10.7 0.7 convert_element_type.133
  11.3 1.5 fusion.20
  13.0 1.5 fusion.31
  14.5 21.0 %gather_fusion = bf16[4096,2048]{1,0:T(8,128)(2,1)} fusion(bf16[256,2048]{1,0:T(8,128)(2,1)S(1)} %fusion.31, s32[4096]{0:T(1024)S(1)} %broadcast_clamp_fusion), kind=kCustom, calls=%fused_computation | custom fusion | bytes 33570816 | tf_op jit(solution)/shard_map/jit(_take)/gather | solution.py:81
  35.5 8.3 %broadcast_select_fusion = bf16[64,64,2048]{2,1,0:T(8,128)(2,1)S(1)} fusion(bf16[64,64,2048]{2,1,0:T(8,128)(2,1)} %bitcast.115, pred[64,64]{1,0:T(8,128)(4,1)S(1)} %compare_and_fusion), kind=kLoop, calls=%fused_computation.7 | loop fusion | flops 8388608 | bytes 33558528 | tf_op jit(solution)/shard_map/jit(_take)/select_n | solution.py:81
  43.8 189.1 %all_to_all.10 = bf16[64,64,2048]{2,1,0:T(8,128)(2,1)S(1)} all-to-all(bf16[64,64,2048]{2,1,0:T(8,128)(2,1)S(1)} %broadcast_select_fusion), channel_id=1, replica_groups=mesh['dp'=2,'ep'=8] {'ep'}, dimensions={0} | all-to-all | bytes 33554432 | tf_op jit(solution)/shard_map/all_to_all | solution.py:82
  232.9 6.6 %copy.46 = bf16[8,8,64,2048]{3,2,1,0:T(8,128)(2,1)} copy(bf16[8,8,64,2048]{3,2,0,1:T(8,128)(2,1)S(1)} %bitcast.117) | data formatting | bytes 33554432 | tf_op jit(solution)/shard_map/transpose | solution.py:83
  239.4 31.9 %fusion.66 = f32[8,512,1024]{2,1,0:T(8,128)} fusion(bf16[8,512,2048]{2,1,0:T(8,128)(2,1)} %bitcast.120, bf16[8,2048,1024]{2,1,0:T(8,128)(2,1)} %param.31), kind=kOutput, calls=%fused_computation.103 | convolution fusion | flops 17179869184 | bytes 67108864 | tf_op jit(solution)/shard_map/ecd,edf->ecf/dot_general | solution.py:59
  271.3 45.4 %convolution_convert_fusion = bf16[8,512,2048]{2,1,0:T(8,128)(2,1)} fusion(bf16[8,1024,2048]{2,1,0:T(8,128)(2,1)} %param.33, f32[8,512,1024]{2,1,0:T(8,128)} %fusion.66, bf16[8,512,2048]{2,1,0:T(8,128)(2,1)} %bitcast.121, bf16[8,2048,1024]{2,1,0:T(8,128)(2,1)} %param.32), kind=kOutput, calls=%fused_computation.8 | convolution fusion | flops 34393292800 | bytes 117440512 | tf_op jit(solution)/shard_map/ecf,efd->ecd/dot_general | solution.py:62
  316.7 14.1 %copy.47 = bf16[8,8,64,2048]{3,2,1,0:T(8,128)(2,1)} copy(bf16[8,8,64,2048]{3,2,0,1:T(8,128)(2,1)} %bitcast.122) | data formatting | bytes 33554432 | tf_op jit(solution)/shard_map/transpose | solution.py:85
  330.8 6.1 all-to-all-start.1
  338.0 16.8 %gather_fusion.2 = f32[2048]{0:T(1024)S(1)} fusion(f32[256,64]{0,1:T(8,128)S(1)} %fusion.65, s32[2048]{0:T(1024)S(1)} %reshape.346), kind=kCustom, calls=%fused_computation.2 | custom fusion | bytes 32768 | tf_op jit(solution)/shard_map/jit(take_along_axis)/gather | solution.py:53
  355.0 6.7 %convolution_convert_fusion.1 = bf16[256,2048]{1,0:T(8,128)(2,1)} fusion(bf16[2048,2048]{1,0:T(8,128)(2,1)} %param.23, bf16[1,256,2048]{2,1,0:T(8,128)(2,1)S(1)} %copy-done.4, f32[2048]{0:T(1024)S(1)} %convert_element_type.119, f32[256]{0:T(256)S(1)} %copy-done.9), kind=kOutput, calls=%fused_computation.31 | convolution fusion | flops 2150105088 | bytes 10494976 | tf_op jit(solution)/shard_map/dot_general | solution.py:35
  361.7 1.5 copy.52
  363.2 12.3 %copy.54 = bf16[2048,2048]{1,0:T(8,128)(2,1)} copy(bf16[2048,2048]{0,1:T(8,128)(2,1)} %bitcast.123) | data formatting | bytes 16777216 | tf_op jit(solution)/shard_map/dot_general | solution.py:33
  375.5 12.3 %copy.53 = bf16[2048,2048]{1,0:T(8,128)(2,1)} copy(bf16[2048,2048]{0,1:T(8,128)(2,1)} %bitcast.124) | data formatting | bytes 16777216 | tf_op jit(solution)/shard_map/dot_general | solution.py:34
  388.5 6.1 convolution_bitcast_fusion
  394.7 2.5 convolution_bitcast_fusion.1
  397.1 0.7 fusion.50
  397.8 0.9 fusion.8
  398.8 0.9 fusion.7
  399.7 1.3 fusion.24
  401.0 1.5 slice-done.1
  402.4 2.5 fusion.17
  405.1 17.3 %fusion.29 = f32[256,8192]{1,0:T(8,128)} fusion(bf16[2048,8192]{1,0:T(8,128)(2,1)} %param.26, bf16[256,2048]{1,0:T(8,128)(2,1)S(1)} %get-tuple-element.20, f32[2048]{0:T(1024)S(1)} %convert_element_type.130, f32[256]{0:T(256)S(1)} %add_rsqrt_fusion), kind=kOutput, calls=%fused_computation.47 | convolution fusion | flops 8592031744 | bytes 43000832 | tf_op jit(solution)/shard_map/dot_general | solution.py:44
  422.4 98.4 %all-to-all-done.1 = bf16[64,64,2048]{2,1,0:T(8,128)(2,1)} async-done(((bf16[64,64,2048]{2,1,0:T(8,128)(2,1)}), bf16[64,64,2048]{2,1,0:T(8,128)(2,1)}, u32[]{:S(2)}, u32[]{:S(2)}) %all-to-all-start.1) | async-done | bytes 16777248 | tf_op jit(solution)/shard_map/all_to_all | solution.py:86
  520.9 50.4 %gather_fusion.1 = bf16[2048,2048]{1,0:T(8,128)(2,1)} fusion(bf16[64,64,2048]{2,1,0:T(8,128)(2,1)} %all-to-all-done.1, s32[2048]{0:T(1024)S(1)} %reshape.340), kind=kCustom, calls=%fused_computation.1 | custom fusion | bytes 16793600 | tf_op jit(solution)/shard_map/gather | solution.py:87
  571.3 11.2 %fusion = f32[256,2048]{1,0:T(8,128)S(1)} fusion(bf16[2048,2048]{1,0:T(8,128)(2,1)} %gather_fusion.1, f32[256,8]{1,0:T(8,128)S(1)} %fusion.52), kind=kLoop, calls=%fused_computation.5 | loop fusion | flops 12058624 | bytes 10493952 | tf_op jit(solution)/shard_map/reduce_sum | solution.py:88
  582.5 29.2 %fusion.14 = bf16[1,256,2048]{2,1,0:T(8,128)(2,1)} fusion(f32[256,2048]{1,0:T(8,128)S(1)} %fusion, bf16[8192,2048]{1,0:T(8,128)(2,1)} %param.28, bf16[2048,8192]{1,0:T(8,128)(2,1)} %param.27, f32[256,8192]{1,0:T(8,128)} %fusion.29, bf16[256,2048]{1,0:T(8,128)(2,1)S(1)} %get-tuple-element.20, f32[2048]{0:T(1024)S(1)} %convert_element_type.130, ...), kind=kOutput, calls=%fused_computation.34 | convolution fusion | flops 17196646400 | bytes 79700992 | tf_op jit(solution)/shard_map/dot_general | solution.py:45
  (62 shorter events, 2.6 us)
Async XLA Ops:
  0.0 337.5 %copy-start = (bf16[2048,64]{0,1:T(8,128)(2,1)S(1)}, bf16[2048,64]{0,1:T(8,128)(2,1)}, u32[]{:S(2)}) copy-start(bf16[2048,64]{0,1:T(8,128)(2,1)} %param.30) | copy-start | bytes 786436
  12.9 22.6 %copy-start.8 = (f32[256]{0:T(256)}, f32[256]{0:T(256)S(1)}, u32[]{:S(2)}) copy-start(f32[256]{0:T(256)S(1)} %add_rsqrt_fusion.1) | copy-start | bytes 3076
  14.5 21.0 %copy-start.2 = (bf16[256,2048]{1,0:T(8,128)(2,1)}, bf16[256,2048]{1,0:T(8,128)(2,1)S(1)}, u32[]{:S(2)}) copy-start(bf16[256,2048]{1,0:T(8,128)(2,1)S(1)} %fusion.31) | copy-start | bytes 3145732
  330.8 6.1 copy-start.5
  330.8 6.2 %copy-start.7 = (s32[256,8,1]{0,1,2:T(8,128)S(1)}, s32[256,8,1]{0,1,2:T(8,128)}, u32[]{:S(2)}) copy-start(s32[256,8,1]{0,1,2:T(8,128)} %get-tuple-element.12) | copy-start | bytes 24580
  330.8 6.5 %copy-start.6 = (s32[256,8,1]{0,1,2:T(8,128)S(1)}, s32[256,8,1]{0,1,2:T(8,128)}, u32[]{:S(2)}) copy-start(s32[256,8,1]{0,1,2:T(8,128)} %get-tuple-element.11) | copy-start | bytes 24580
  330.8 6.7 %copy-start.3 = (bf16[256,2048]{1,0:T(8,128)(2,1)S(1)}, bf16[256,2048]{1,0:T(8,128)(2,1)}, u32[]{:S(2)}) copy-start(bf16[256,2048]{1,0:T(8,128)(2,1)} %copy-done.2) | copy-start | bytes 3145732
  330.8 190.0 %all-to-all-start.1 = ((bf16[64,64,2048]{2,1,0:T(8,128)(2,1)}), bf16[64,64,2048]{2,1,0:T(8,128)(2,1)}, u32[]{:S(2)}, u32[]{:S(2)}) async-start(bf16[64,64,2048]{2,1,0:T(8,128)(2,1)} %bitcast.116), calls=%async_computation.1 | async-start | bytes 33554432 | tf_op jit(solution)/shard_map/all_to_all | solution.py:86
  338.0 16.9 %copy-start.10 = (bf16[2048]{0:T(1024)(128)(2,1)S(1)}, bf16[2048]{0:T(1024)(128)(2,1)}, u32[]{:S(2)}) copy-start(bf16[2048]{0:T(1024)(128)(2,1)} %param.20) | copy-start | bytes 12292
  338.0 16.9 %copy-start.4 = (bf16[1,256,2048]{2,1,0:T(8,128)(2,1)S(1)}, bf16[1,256,2048]{2,1,0:T(8,128)(2,1)}, u32[]{:S(2)}) copy-start(bf16[1,256,2048]{2,1,0:T(8,128)(2,1)} %param.17) | copy-start | bytes 3145732
  338.0 16.9 %copy-start.9 = (f32[256]{0:T(256)S(1)}, f32[256]{0:T(256)}, u32[]{:S(2)}) copy-start(f32[256]{0:T(256)} %copy-done.8) | copy-start | bytes 3076
  375.5 12.3 %copy-start.11 = (bf16[2048]{0:T(1024)(128)(2,1)S(1)}, bf16[2048]{0:T(1024)(128)(2,1)}, u32[]{:S(2)}) copy-start(bf16[2048]{0:T(1024)(128)(2,1)} %param.25) | copy-start | bytes 12292
  388.0 6.6 %slice-start.2 = ((s8[8388608]{0:T(1024)(128)(4,1)}), s8[4194304]{0:T(1024)(128)(4,1)S(1)}, s32[]{:S(2)}) async-start(s8[8388608]{0:T(1024)(128)(4,1)} %bitcast.125), calls=%async_computation.4 | async-start | bytes 8388608
  388.5 6.1 %slice-start.3 = ((s8[8388608]{0:T(1024)(128)(4,1)}), s8[4194304]{0:T(1024)(128)(4,1)S(1)}, s32[]{:S(2)}) async-start(s8[8388608]{0:T(1024)(128)(4,1)} %bitcast.125), calls=%async_computation.5 | async-start | bytes 8388608
  398.7 2.2 slice-start
  399.7 2.8 slice-start.1
  582.4 29.2 %copy-start.1 = (bf16[2048,64]{0,1:T(8,128)(2,1)S(1)}, bf16[2048,64]{0,1:T(8,128)(2,1)}, u32[]{:S(2)}) copy-start(bf16[2048,64]{0,1:T(8,128)(2,1)} %param.30) | copy-start | bytes 786436
where the time goes:
time: 622 us; the launch traced here: 612 us
  blocking collectives  189 us (30%)
  local copies, waits for them, and re-layouts  146 us (23%)
  matrix products  144 us (23%)
  waiting for transfers between devices  98.4 us (16%)
  other arithmetic  27.7 us (4%)
    all_to_all x1, blocking collectives, local(): recv = lax.all_to_all(send, 'ep', 0, 0, tiled=True)  189 us
    all_to_all x1, waiting for transfers between devices, local(): back = lax.all_to_all(y, 'ep', 0, 0, tiled=True)  98.4 us
    gather x1, local copies, waits for them, and re-layouts, local(): yg = back[ix, sl]  50.4 us
    dot_general x1, matrix products, _experts(): jnp.einsum('ecf,efd->ecd', hid, ue2, preferred_element_type=f32)  45.4 us
    dot_general x1, matrix products, _experts(): h1 = jnp.einsum('ecd,edf->ecf', x, ue1, preferred_element_type=f32)  31.9 us
    dot_general x1, matrix products, _dense(): return a.astype(f32) + jnp.dot(hid, w2, preferred_element_type=f32)  29.2 us
    gather x1, local copies, waits for them, and re-layouts, local(): send = jnp.take(u, tok, axis=0, mode='fill', fill_value=0)  21 us
    dot_general x1, matrix products, _dense(): jnp.dot(z, w1, preferred_element_type=f32)  17.3 us
  transfers between devices with their start and end apart: 1, of which 1 were waited for; matrix products, arithmetic and copies ran while one was open for 14% of the time, Pallas kernels for 0%

commit v1 on v0

v1 whole, which is shorter than its diff:
```python
import functools

import jax
import jax.numpy as jnp
from jax import lax
from jax.experimental import pallas as pl
from jax.experimental.pallas import tpu as pltpu
from jax.sharding import PartitionSpec as P

HEAD = 128
EPS = 1e-6
ROPE_BASE = 10000.0
F32, BF = jnp.float32, jnp.bfloat16


def _rms(x, w):
    xf = x.astype(F32)
    r = lax.rsqrt(jnp.mean(xf * xf, axis=-1, keepdims=True) + EPS)
    return (xf * r * w.astype(F32)).astype(BF)


def _dot(a, b):
    return jnp.dot(a, b, preferred_element_type=F32)


def _attn_kernel(h_ref, na_ref, cos_ref, sin_ref, wq_ref, wk_ref, wv_ref, wo_ref, a_ref, x_sc, acc_sc, *, nsteps, hps):
    i = pl.program_id(0)
    t = h_ref.shape[0]

    @pl.when(i == 0)
    def _():
        x_sc[...] = _rms(h_ref[...], na_ref[...])
        acc_sc[...] = jnp.zeros_like(acc_sc)

    x = x_sc[...]
    q2 = _dot(x, wq_ref[...])
    k2 = _dot(x, wk_ref[...])
    v2 = _dot(x, wv_ref[...]).astype(BF)
    cos, sin = cos_ref[...], sin_ref[...]
    causal = lax.broadcasted_iota(jnp.int32, (t, t), 0) >= lax.broadcasted_iota(jnp.int32, (t, t), 1)
    outs = []
    for h in range(hps):
        sl = slice(h * HEAD, (h + 1) * HEAD)
        q, k, v = q2[:, sl], k2[:, sl], v2[:, sl]
        q = (q * cos + pltpu.roll(q, HEAD // 2, 1) * sin).astype(BF)
        k = (k * cos + pltpu.roll(k, HEAD // 2, 1) * sin).astype(BF)
        s = lax.dot_general(q, k, (((1,), (1,)), ((), ())), preferred_element_type=F32) * HEAD ** -0.5
        s = jnp.where(causal, s, -jnp.inf)
        p = jnp.exp(s - jnp.max(s, axis=-1, keepdims=True))
        p = (p / jnp.sum(p, axis=-1, keepdims=True)).astype(BF)
        outs.append(_dot(p, v).astype(BF))
    o = jnp.concatenate(outs, axis=1)
    acc_sc[...] += _dot(o, wo_ref[...])

    @pl.when(i == nsteps - 1)
    def _():
        a_ref[...] = (h_ref[...].astype(F32) + acc_sc[...]).astype(BF)


def _attention(h, na, wq, wk, wv, wo):
    t, d = h.shape
    hps = 2
    nsteps = wq.shape[1] // (HEAD * hps)
    w = HEAD * hps
    pos = jnp.arange(t).astype(F32)
    inv = ROPE_BASE ** (-2.0 * jnp.arange(HEAD // 2).astype(F32) / HEAD)
    ang = pos[:, None] * inv[None, :]
    c, s = jnp.cos(ang), jnp.sin(ang)
    cos, sin = jnp.concatenate([c, c], 1), jnp.concatenate([-s, s], 1)
    full = lambda shape: pl.BlockSpec(shape, lambda i: (0, 0))
    return pl.pallas_call(
        functools.partial(_attn_kernel, nsteps=nsteps, hps=hps),
        grid=(nsteps,),
        in_specs=[full((t, d)), full((1, d)), full((t, HEAD)), full((t, HEAD))]
        + [pl.BlockSpec((d, w), lambda i: (0, i))] * 3
        + [pl.BlockSpec((w, d), lambda i: (i, 0))],
        out_specs=full((t, d)),
        out_shape=jax.ShapeDtypeStruct((t, d), BF),
        scratch_shapes=[pltpu.VMEM((t, d), BF), pltpu.VMEM((t, d), F32)],
        cost_estimate=pl.CostEstimate(flops=8 * t * d * d, bytes_accessed=8 * d * d, transcendentals=0),
        compiler_params=pltpu.CompilerParams(dimension_semantics=("arbitrary",)),
        name="attn",
    )(h, na.reshape(1, d), cos, sin, wq, wk, wv, wo)


def _ffn_kernel(a_ref, nf_ref, w1_ref, w3_ref, w2_ref, o_ref, z_sc, *, nsteps):
    i = pl.program_id(0)

    @pl.when(i == 0)
    def _():
        z_sc[...] = _rms(a_ref[...], nf_ref[...])
        o_ref[...] = a_ref[...].astype(F32)

    z = z_sc[...]
    h1 = _dot(z, w1_ref[...])
    h3 = _dot(z, w3_ref[...])
    hid = (h1 * jax.nn.sigmoid(h1) * h3).astype(BF)
    o_ref[...] += _dot(hid, w2_ref[...])


def _ffn(a, nf, w1, w3, w2):
    t, d = a.shape
    ff = w1.shape[1]
    ft = 512
    nsteps = ff // ft
    full = lambda shape: pl.BlockSpec(shape, lambda i: (0, 0))
    return pl.pallas_call(
        functools.partial(_ffn_kernel, nsteps=nsteps),
        grid=(nsteps,),
        in_specs=[full((t, d)), full((1, d))]
        + [pl.BlockSpec((d, ft), lambda i: (0, i))] * 2
        + [pl.BlockSpec((ft, d), lambda i: (i, 0))],
        out_specs=full((t, d)),
        out_shape=jax.ShapeDtypeStruct((t, d), F32),
        scratch_shapes=[pltpu.VMEM((t, d), BF)],
        cost_estimate=pl.CostEstimate(flops=6 * t * d * ff, bytes_accessed=6 * d * ff, transcendentals=0),
        compiler_params=pltpu.CompilerParams(dimension_semantics=("arbitrary",)),
        name="ffn",
    )(a, nf.reshape(1, d), w1, w3, w2)


def _expert_kernel(off_ref, nb_ref, u_ref, rt_ref, r_ref, g_ref, w1_ref, w3_ref, w2_ref, o_ref,
                   x_sc, acc_sc, y_sc, *, ns, el, cap, nf, mb):
    i = pl.program_id(0)
    d = u_ref.shape[-1]
    t = u_ref.shape[1]
    rows = ns * cap

    @pl.when(i < ns)
    def _():
        it = lax.broadcasted_iota(jnp.int32, (cap, t), 0)
        p = jnp.concatenate(
            [jnp.where(it == rt_ref[0, e:e + 1, :], 1.0, 0.0).astype(BF) for e in range(el)], axis=0)
        for c in range(d // 512):
            cs = slice(c * 512, (c + 1) * 512)
            xv = _dot(p, u_ref[0, :, cs]).astype(BF)
            for e in range(el):
                o = pl.multiple_of(off_ref[i * el + e], 16)
                x_sc[e, pl.ds(o, cap), cs] = xv[e * cap:(e + 1) * cap]

    j = i - ns
    for m in range(mb, rows + 1, mb):
        e = lax.div(jnp.maximum(j, 0), nf)

        @pl.when((j >= 0) & (j < el * nf) & (nb_ref[jnp.minimum(e, el - 1)] == m // mb))
        def _():
            f = lax.rem(j, nf)
            x = x_sc[e, :m, :]
            h1 = _dot(x, w1_ref[0])
            h3 = _dot(x, w3_ref[0])
            hid = (h1 * jax.nn.sigmoid(h1) * h3).astype(BF)
            y = _dot(hid, w2_ref[0])

            @pl.when(f == 0)
            def _():
                acc_sc[:m, :] = y

            @pl.when(f == nf - 1)
            def _():
                x_sc[e, :m, :] = (acc_sc[:m, :] + y).astype(BF)

    s = j - el * nf

    @pl.when(s >= 0)
    def _():
        for e in range(el):
            o = pl.multiple_of(off_ref[s * el + e], 16)
            y_sc[e * cap:(e + 1) * cap, :] = x_sc[e, pl.ds(o, cap), :]
        r, g = r_ref[0], g_ref[0]
        per = 128 // cap
        lane = lax.broadcasted_iota(jnp.int32, (t, 128), 1)
        parts = []
        for q in range(el // per):
            rr, gg = r[:, q * per:q * per + 1], g[:, q * per:q * per + 1]
            for k in range(1, per):
                hit = lane >= k * cap
                rr = jnp.where(hit, r[:, q * per + k:q * per + k + 1], rr)
                gg = jnp.where(hit, g[:, q * per + k:q * per + k + 1], gg)
            parts.append(jnp.where(rr == lane % cap, gg, 0.0))
        gm = jnp.concatenate(parts, axis=1)
        ghi = gm.astype(BF)
        r1 = gm - ghi.astype(F32)
        gmid = r1.astype(BF)
        glo = (r1 - gmid.astype(F32)).astype(BF)
        for c in range(d // 512):
            cs = slice(c * 512, (c + 1) * 512)
            y = y_sc[:, cs]
            o_ref[0, :, cs] = _dot(ghi, y) + (_dot(gmid, y) + _dot(glo, y))


def _experts(u_all, gm, ue1, ue3, ue2, cap):
    ns, t, d = u_all.shape
    el, _, fe = ue1.shape
    mb, nf = 128, 2
    ft = fe // nf
    routed = gm >= 0
    before = (jnp.arange(t)[:, None] > jnp.arange(t)[None, :]).astype(BF)
    rank = jnp.einsum('ab,sbe->sae', before, routed.astype(BF), preferred_element_type=F32).astype(jnp.int32)
    rank = jnp.where(routed, rank, -1)
    cnt = jnp.sum(routed.astype(jnp.int32), axis=1)
    pad = (cnt + 15) // 16 * 16
    off = jnp.cumsum(pad, axis=0) - pad
    nb = jnp.maximum((jnp.sum(pad, axis=0) + mb - 1) // mb, 1)
    steps = ns + el * nf + ns
    wi = lambda i: jnp.clip(i - ns, 0, el * nf - 1)
    gs = pltpu.PrefetchScalarGridSpec(
        num_scalar_prefetch=2,
        grid=(steps,),
        in_specs=[
            pl.BlockSpec((1, t, d), lambda i, *_: (jnp.minimum(i, ns - 1), 0, 0)),
            pl.BlockSpec((1, el, t), lambda i, *_: (jnp.minimum(i, ns - 1), 0, 0)),
            pl.BlockSpec((1, t, el), lambda i, *_: (jnp.maximum(i - ns - el * nf, 0), 0, 0)),
            pl.BlockSpec((1, t, el), lambda i, *_: (jnp.maximum(i - ns - el * nf, 0), 0, 0)),
            pl.BlockSpec((1, d, ft), lambda i, *_: (wi(i) // nf, 0, wi(i) % nf)),
            pl.BlockSpec((1, d, ft), lambda i, *_: (wi(i) // nf, 0, wi(i) % nf)),
            pl.BlockSpec((1, ft, d), lambda i, *_: (wi(i) // nf, wi(i) % nf, 0)),
        ],
        out_specs=pl.BlockSpec((1, t, d), lambda i, *_: (jnp.maximum(i - ns - el * nf, 0), 0, 0)),
        scratch_shapes=[
            pltpu.VMEM((el, ns * cap, d), BF),
            pltpu.VMEM((ns * cap, d), F32),
            pltpu.VMEM((el * cap, d), BF),
        ],
    )
    return pl.pallas_call(
        functools.partial(_expert_kernel, ns=ns, el=el, cap=cap, nf=nf, mb=mb),
        grid_spec=gs,
        out_shape=jax.ShapeDtypeStruct((ns, t, d), F32),
        cost_estimate=pl.CostEstimate(flops=6 * el * ns * cap * d * fe, bytes_accessed=6 * el * d * fe, transcendentals=0),
        compiler_params=pltpu.CompilerParams(dimension_semantics=("arbitrary",), vmem_limit_bytes=60 << 20),
        name="experts",
    )(off.reshape(-1), nb, u_all, rank.transpose(0, 2, 1), rank, gm, ue1, ue3, ue2)


def solution(mesh):
    G = mesh.shape['ep']

    def local(h0, idx, slot, na, wq, wk, wv, wo, nf, w1, w3, w2, nm, wr, ue1, ue3, ue2):
        b, s, d = h0.shape
        t = b * s
        k = idx.shape[-1]
        el = ue1.shape[0]
        ne = el * G
        cap = 2 * t * k // ne
        h = h0.reshape(t, d)
        u = _rms(h, nm)
        logits = _dot(u, wr)
        ix = idx.reshape(t, k)
        hot = ix[:, :, None] == jnp.arange(ne)[None, None, :]
        routed = jnp.any(hot, axis=1)
        lg = jnp.where(routed, logits, -jnp.inf)
        mx = jnp.max(lg, axis=-1, keepdims=True)
        ex = jnp.exp(lg - mx)
        g = ex / jnp.sum(ex, axis=-1, keepdims=True)
        gm = jnp.where(routed, g, -1.0)
        u_all = lax.all_gather(u, 'ep')
        gm_all = lax.all_gather(gm, 'ep')
        me = lax.axis_index('ep')
        gm_loc = lax.dynamic_slice_in_dim(gm_all, me * el, el, axis=2)
        a = _attention(h, na, wq, wk, wv, wo)
        part = _experts(u_all, gm_loc, ue1, ue3, ue2, cap)
        m = lax.psum_scatter(part, 'ep', scatter_dimension=0)
        dense = _ffn(a, nf, w1, w3, w2)
        return (dense + m.reshape(t, d)).astype(BF).reshape(b, s, d)

    rows_spec = P(('dp', 'ep'))
    in_specs = (rows_spec,) * 3 + (P(),) * 11 + (P('ep'),) * 3
    return jax.shard_map(local, mesh=mesh, in_specs=in_specs, out_specs=rows_spec, check_vma=False)
```

time: 622 us -> 268 us (0.43); the launches traced: 612 us -> 268 us
  blocking collectives: 189 us -> 11.7 us
  Pallas kernels: 0 us -> 150 us
  matrix products: 144 us -> 0.82 us
  local copies, waits for them, and re-layouts: 146 us -> 3.61 us
  waiting for transfers between devices: 98.4 us -> 74.4 us
  other arithmetic: 27.7 us -> 13.6 us
  between operations: 0.78 us -> 13.5 us
    all_to_all x1 -> x0, blocking collectives: 189 us -> none  [local(): recv = lax.all_to_all(send, 'ep', 0, 0, tiled=True)]
    pallas_call x0 -> x3, Pallas kernels: none -> 150 us  [the longest x1 83.3 us: _experts(): pl.pallas_call(functools.partial(_expert_kernel, ns=ns, el=el, cap=cap, n...]
    dot_general x11 -> x2, matrix products: 144 us -> 0.82 us  [the longest x1 0.52 us: _dot(): return jnp.dot(a, b, preferred_element_type=F32)]
    all_to_all x1 -> x0, waiting for transfers between devices: 98.4 us -> none  [local(): back = lax.all_to_all(y, 'ep', 0, 0, tiled=True)]
    gather x6 -> x0, local copies, waits for them, and re-layouts: 88.5 us -> none  [the longest x1 50.4 us: local(): yg = back[ix, sl]]
    reduce_scatter x0 -> x1, waiting for transfers between devices: none -> 39.4 us  [local(): m = lax.psum_scatter(part, 'ep', scatter_dimension=0)]
    all_gather x0 -> x1, waiting for transfers between devices: none -> 34.9 us  [local(): u_all = lax.all_gather(u, 'ep')]
    dot_general x2 -> x0, local copies, waits for them, and re-layouts: 24.6 us -> none  [the longest x1 12.3 us: _dense(): jnp.dot(x, wk, preferred_element_type=f32).reshape(b, s, nkvv, HEAD)]
  transfers between devices with their start and end apart: 1 -> 2, of which waited for: 1 -> 2; matrix products, arithmetic and copies ran while one was open for 14% -> 3% of each run, Pallas kernels for 0% -> 25%
where the time goes in v1:
time: 268 us
  Pallas kernels  150 us (56%)
  waiting for transfers between devices  74.4 us (28%)
  other arithmetic  13.6 us (5%)
  between operations  13.5 us (5%)
  blocking collectives  11.7 us (4%)
  local copies, waits for them, and re-layouts  3.61 us (1%)
    pallas_call x1, Pallas kernels, _experts(): pl.pallas_call(functools.partial(_expert_kernel, ns=ns, el=el, cap=cap, n...  83.3 us
    pallas_call x1, Pallas kernels, _ffn(): pl.pallas_call(functools.partial(_ffn_kernel, nsteps=nsteps), grid=(nstep...  43.8 us
    reduce_scatter x1, waiting for transfers between devices, local(): m = lax.psum_scatter(part, 'ep', scatter_dimension=0)  39.4 us
    all_gather x1, waiting for transfers between devices, local(): u_all = lax.all_gather(u, 'ep')  34.9 us
    pallas_call x1, Pallas kernels, _attention(): pl.pallas_call(functools.partial(_attn_kernel, nsteps=nsteps, hps=hps), g...  23.4 us
    all_gather x1, blocking collectives, local(): gm_all = lax.all_gather(gm, 'ep')  11.7 us
  transfers between devices with their start and end apart: 2, of which 2 were waited for; matrix products, arithmetic and copies ran while one was open for 3% of the time, Pallas kernels for 25%

profile of v1, /device:TPU:0, one launch (start us, length us, event | category | flops | bytes accessed | tf_op | source)
XLA Modules:
  0.0 268.0 jit_solution(3862954881864793417)
XLA Ops:
  6.5 0.0 all-gather.3.cloned.1.call-start
  6.5 0.7 convert_element_type.58
  7.3 1.6 fusion
  8.9 2.5 multiply_convert_fusion
  11.4 0.0 all-gather.3.cloned.1.call-update
  11.4 0.0 reduce-scatter.2.cloned.1.call-start
  11.5 0.1 fusion.9
  11.6 0.0 copy-done
  11.6 0.5 fusion.22
  12.2 11.7 %all-gather = f32[2048,64]{0,1:T(8,128)S(1)} all-gather(f32[256,64]{0,1:T(8,128)S(1)} %divide_select_fusion), channel_id=2, replica_groups=mesh['dp'=2,'ep'=8] {'ep'}, dimensions={0}, use_global_device_ids=true | all-gather | bytes 589824 | tf_op jit(solution)/shard_map/all_gather | solution.py:257
  23.9 0.3 copy.31
  24.2 1.3 convert_reduce_fusion
  25.6 0.1 reduce_window_sum.14
  25.6 0.1 add.43
  25.7 0.3 convolution_convert_fusion
  26.0 0.3 copy.33
  26.4 1.3 bitcast_select_fusion
  27.6 0.9 copy.34.rt_ref
  28.6 0.6 fusion.18.nb_ref
  29.1 0.5 multiply_subtract_fusion.off_ref
  29.7 34.9 %all-gather.3.cloned.1.call-done.u_ref = bf16[8,256,2048]{2,1,0:T(8,128)(2,1)} async-done(((bf16[1,256,2048]{2,1,0:T(8,128)(2,1)}), bf16[8,256,2048]{2,1,0:T(8,128)(2,1)}) %all-gather.3.cloned.1.call-update) | async-done | bytes 8388624 | tf_op jit(solution)/shard_map/all_gather | solution.py:256
  64.6 83.3 %experts.1 = f32[8,256,2048]{2,1,0:T(8,128)} custom-call(s32[64]{0:T(128)} %multiply_subtract_fusion.off_ref, s32[8]{0:T(128)} %fusion.18.nb_ref, bf16[8,256,2048]{2,1,0:T(8,128)(2,1)} %all-gather.3.cloned.1.call-done.u_ref, s32[8,8,256]{2,1,0:T(8,128)} %copy.34.rt_ref, s32[8,256,8]{2,1,0:T(8,128)} %get-tuple-element.10.r_ref, ...), custom_call_target="tpu_custom_call" | custom-call | flops 51539607552 | bytes 100663296 | tf_op jit(solution)/shard_map/experts/pallas_call | solution.py:225
  147.9 0.0 reduce-scatter.2.cloned.1.call-update
  147.9 0.7 copy-done.4
  148.6 0.6 reshape.52.na_ref
  149.2 0.6 reshape.53.nf_ref
  149.8 0.5 fusion.14
  150.3 0.9 pad_maximum_fusion
  151.2 23.4 %attn.1.a_ref = bf16[256,2048]{1,0:T(8,128)(2,1)} custom-call(bf16[256,2048]{1,0:T(8,128)(2,1)} %bitcast.28, bf16[1,2048]{1,0:T(2,128)(2,1)} %reshape.52.na_ref, f32[256,128]{1,0:T(8,128)} %get-tuple-element.18.cos_ref, f32[256,128]{1,0:T(8,128)} %get-tuple-element.19.sin_ref, bf16[2048,2048]{1,0:T(8,128)(2,1)} %wq_ref.1, bf16[2048,2048]{1,0:T(8,128)(2,1)} %wk_ref.1, ...), custom_call_target="tpu_custom_call" | custom-call | flops 8589934592 | bytes 33554432 | tf_op jit(solution)/shard_map/attn/pallas_call | solution.py:71
  174.5 43.8 %ffn.1 = f32[256,2048]{1,0:T(8,128)} custom-call(bf16[256,2048]{1,0:T(8,128)(2,1)} %attn.1.a_ref, bf16[1,2048]{1,0:T(2,128)(2,1)} %reshape.53.nf_ref, bf16[2048,8192]{1,0:T(8,128)(2,1)} %w1_ref.2, bf16[2048,8192]{1,0:T(8,128)(2,1)} %w3_ref.2, bf16[8192,2048]{1,0:T(8,128)(2,1)} %w2_ref.2), custom_call_target="tpu_custom_call" | custom-call | flops 25769803776 | bytes 100663296 | tf_op jit(solution)/shard_map/ffn/pallas_call | solution.py:107
  218.3 39.4 %reduce-scatter.2.cloned.1.call-done = f32[1,256,2048]{2,1,0:T(8,128)} async-done(((f32[8,256,2048]{2,1,0:T(8,128)}), f32[1,256,2048]{2,1,0:T(8,128)}) %reduce-scatter.2.cloned.1.call-update) | async-done | bytes 2097168 | tf_op jit(solution)/shard_map/reduce_scatter | solution.py:262
  257.7 3.5 %fusion.4 = bf16[1,256,2048]{2,1,0:T(8,128)(2,1)} fusion(f32[256,2048]{1,0:T(8,128)} %ffn.1, f32[1,256,2048]{2,1,0:T(8,128)} %reduce-scatter.2.cloned.1.call-done), kind=kLoop, calls=%fused_computation.10 | loop fusion | flops 1048576 | bytes 5242880 | tf_op jit(solution)/shard_map/reshape | solution.py:264
  (17 shorter events, 0.1 us)
Async XLA Ops:
  6.5 5.0 %copy-start = (bf16[2048,64]{0,1:T(8,128)(2,1)S(1)}, bf16[2048,64]{0,1:T(8,128)(2,1)}, u32[]{:S(2)}) copy-start(bf16[2048,64]{0,1:T(8,128)(2,1)} %param.29) | copy-start | bytes 786436
  6.5 58.0 %all-gather.3.cloned.1.call-start = ((), (), s32[]{:S(2)}) async-start(), calls=%async_computation.1 | async-start | bytes 9437184 | tf_op jit(solution)/shard_map/all_gather | solution.py:256
  7.3 4.2 %copy-start.3 = (s32[1,256,8]{1,2,0:T(8,128)S(1)}, s32[1,256,8]{1,2,0:T(8,128)}, u32[]{:S(2)}) copy-start(s32[1,256,8]{1,2,0:T(8,128)} %param.18) | copy-start | bytes 24580
  7.3 4.3 %copy-start.2 = (bf16[1,256,2048]{2,1,0:T(8,128)(2,1)S(1)}, bf16[1,256,2048]{2,1,0:T(8,128)(2,1)}, u32[]{:S(2)}) copy-start(bf16[1,256,2048]{2,1,0:T(8,128)(2,1)} %param.17) | copy-start | bytes 3145732
  11.4 246.3 %reduce-scatter.2.cloned.1.call-start = ((), (), s32[]{:S(2)}) async-start(), calls=%async_computation.2 | async-start | bytes 18874368 | tf_op jit(solution)/shard_map/reduce_scatter | solution.py:262
  147.9 0.7 copy-start.4
  147.9 1.3 copy-start.5
  174.5 86.6 %copy-start.1 = (bf16[2048,64]{0,1:T(8,128)(2,1)S(1)}, bf16[2048,64]{0,1:T(8,128)(2,1)}, u32[]{:S(2)}) copy-start(bf16[2048,64]{0,1:T(8,128)(2,1)} %param.29) | copy-start | bytes 786436
Sparse Core Ops, SparseCore 0:
  11.6 52.9 all-gather.2
  148.0 109.6 reduce-scatter.1

commit v2 on v0

v2 whole, which is shorter than its diff:
```python
import functools

import jax
import jax.numpy as jnp
from jax import lax
from jax.experimental import pallas as pl
from jax.experimental.pallas import tpu as pltpu
from jax.sharding import PartitionSpec as P

HEAD = 128
EPS = 1e-6
ROPE_BASE = 10000.0
F32, BF = jnp.float32, jnp.bfloat16


def _rms(x, w):
    xf = x.astype(F32)
    r = lax.rsqrt(jnp.mean(xf * xf, axis=-1, keepdims=True) + EPS)
    return (xf * r * w.astype(F32)).astype(BF)


def _dot(a, b):
    return jnp.dot(a, b, preferred_element_type=F32)


MESH = pl.DeviceIdType.MESH


def _peer(me, r):
    p = me
    if r & 1:
        p = p + 1 - 2 * (me % 2)
    if r & 2:
        p = p + 2 - 4 * ((me // 2) % 2)
    if r & 4:
        p = p + 4 - 8 * (me // 4)
    return p


def _barrier(me, rels):
    sem = pltpu.get_barrier_semaphore()
    for r in rels:
        pl.semaphore_signal(sem, inc=1, device_id={'ep': _peer(me, r)}, device_id_type=MESH)
    return lambda: pl.semaphore_wait(sem, len(rels))


def _ffn_tile(z, w1, w3, w2):
    h1 = _dot(z, w1)
    h3 = _dot(z, w3)
    hid = (h1 * jax.nn.sigmoid(h1) * h3).astype(BF)
    return _dot(hid, w2)


def _first_kernel(h_ref, na_ref, nm_ref, nf_ref, wr_ref, idx_ref, cos_ref, sin_ref, wq_ref, wk_ref, wv_ref, wo_ref,
                  w1_ref, w3_ref, w2_ref, z_ref, f_ref, uall_ref, gall_ref,
                  x_sc, acc_sc, u_sc, g_sc, sa, ra, sb, rb, sc, rc, sg, rg, ls, *, na_steps, nf_steps, hps, el, step_b, step_c):
    i = pl.program_id(0)
    t, d = h_ref.shape
    me = lax.axis_index('ep')
    hops = (1, 2, 4)
    half = t // 2

    def remote(src, dst, s, r, rel):
        return pltpu.make_async_remote_copy(src_ref=src, dst_ref=dst, send_sem=s, recv_sem=r,
                                            device_id={'ep': _peer(me, rel)}, device_id_type=MESH)

    def stage_a(n):
        return remote(u_sc, uall_ref.at[hops[n]], sa.at[n], ra.at[n], hops[n])

    def stage_g(r):
        rows = pl.ds(pl.multiple_of(_peer(me, r) * el, el), el)
        return remote(g_sc.at[rows], gall_ref.at[r], sg.at[r - 1], rg.at[r - 1], r)

    def stage_b(n):
        rows = pl.ds(n * half, half)
        return remote(uall_ref.at[(2, 4)[n], rows], uall_ref.at[6, rows], sb.at[n], rb.at[n], (4, 2)[n])

    def stage_c(n):
        return remote(uall_ref.at[2 * n + 2], uall_ref.at[2 * n + 3], sc.at[n], rc.at[n], 1)

    def own():
        rows = pl.ds(pl.multiple_of(me * el, el), el)
        return (pltpu.make_async_copy(u_sc, uall_ref.at[0], ls.at[0]),
                pltpu.make_async_copy(g_sc.at[rows], gall_ref.at[0], ls.at[1]))

    @pl.when(i == 0)
    def _():
        arrived = _barrier(me, range(1, 8))
        u = _rms(h_ref[...], nm_ref[...])
        u_sc[...] = u
        logits = _dot(u, wr_ref[...])
        ne = logits.shape[1]
        lane = lax.broadcasted_iota(jnp.int32, (t, ne), 1)
        routed = lane == idx_ref[:, 0:1]
        for j in range(1, idx_ref.shape[1]):
            routed = routed | (lane == idx_ref[:, j:j + 1])
        lg = jnp.where(routed, logits, -jnp.inf)
        ex = jnp.exp(lg - jnp.max(lg, axis=-1, keepdims=True))
        g = jnp.where(routed, ex / jnp.sum(ex, axis=-1, keepdims=True), -1.0)
        g_sc[...] = jnp.transpose(jnp.concatenate([g] * (128 // ne), axis=1))[:ne]
        arrived()
        for n in (1, 2, 0):
            stage_a(n).start()
        for r in range(1, 8):
            stage_g(r).start()
        for c in own():
            c.start()
        x_sc[...] = _rms(h_ref[...], na_ref[...])
        acc_sc[...] = jnp.zeros_like(acc_sc)

    @pl.when(i < na_steps)
    def _():
        x = x_sc[...]
        q2 = _dot(x, wq_ref[...])
        k2 = _dot(x, wk_ref[...])
        v2 = _dot(x, wv_ref[...]).astype(BF)
        cos, sin = cos_ref[...], sin_ref[...]
        causal = lax.broadcasted_iota(jnp.int32, (t, t), 0) >= lax.broadcasted_iota(jnp.int32, (t, t), 1)
        outs = []
        for h in range(hps):
            sl = slice(h * HEAD, (h + 1) * HEAD)
            q, k, v = q2[:, sl], k2[:, sl], v2[:, sl]
            q = (q * cos + pltpu.roll(q, HEAD // 2, 1) * sin).astype(BF)
            k = (k * cos + pltpu.roll(k, HEAD // 2, 1) * sin).astype(BF)
            s = lax.dot_general(q, k, (((1,), (1,)), ((), ())), preferred_element_type=F32) * HEAD ** -0.5
            s = jnp.where(causal, s, -jnp.inf)
            p = jnp.exp(s - jnp.max(s, axis=-1, keepdims=True))
            p = (p / jnp.sum(p, axis=-1, keepdims=True)).astype(BF)
            outs.append(_dot(p, v).astype(BF))
        acc_sc[...] += _dot(jnp.concatenate(outs, axis=1), wo_ref[...])

    @pl.when(i == na_steps - 1)
    def _():
        a = (h_ref[...].astype(F32) + acc_sc[...]).astype(BF)
        f_ref[...] = a.astype(F32)
        z_ref[...] = _rms(a, nf_ref[...])

    @pl.when(i == step_b)
    def _():
        for n in range(2):
            stage_a(n + 1).wait_recv()
            stage_b(n).start()
            stage_c(n).start()

    @pl.when(i == step_c)
    def _():
        for n in range(2):
            stage_b(n).wait_recv()
        stage_c(2).start()

    @pl.when(i >= na_steps)
    def _():
        f_ref[...] += _ffn_tile(z_ref[...], w1_ref[...], w3_ref[...], w2_ref[...])

    @pl.when(i == na_steps + nf_steps - 1)
    def _():
        stage_a(0).wait_recv()
        for n in range(3):
            stage_a(n).wait_send()
        for n in range(2):
            stage_b(n).wait_send()
        for n in range(3):
            stage_c(n).wait()
        for r in range(1, 8):
            stage_g(r).wait()
        for c in own():
            c.wait()


def _first(h, na, nm, nf, wr, idx, wq, wk, wv, wo, w1, w3, w2, el, nf_steps, ft):
    t, d = h.shape
    hps = 2
    w = HEAD * hps
    na_steps = wq.shape[1] // w
    ne = wr.shape[1]
    pos = jnp.arange(t).astype(F32)
    inv = ROPE_BASE ** (-2.0 * jnp.arange(HEAD // 2).astype(F32) / HEAD)
    ang = pos[:, None] * inv[None, :]
    c, s = jnp.cos(ang), jnp.sin(ang)
    cos, sin = jnp.concatenate([c, c], 1), jnp.concatenate([-s, s], 1)
    full = lambda shape: pl.BlockSpec(shape, lambda i: (0, 0))
    ai = lambda i: jnp.minimum(i, na_steps - 1)
    fi = lambda i: jnp.maximum(i - na_steps, 0)
    any_ = pl.BlockSpec(memory_space=pl.ANY)
    dma = pltpu.SemaphoreType.DMA
    return pl.pallas_call(
        functools.partial(_first_kernel, na_steps=na_steps, nf_steps=nf_steps, hps=hps, el=el, step_b=na_steps + 1,
                          step_c=na_steps + nf_steps - 2),
        grid=(na_steps + nf_steps,),
        in_specs=[full((t, d)), full((1, d)), full((1, d)), full((1, d)), full((d, ne)), full(idx.shape),
                  full((t, HEAD)), full((t, HEAD))]
        + [pl.BlockSpec((d, w), lambda i: (0, ai(i)))] * 3
        + [pl.BlockSpec((w, d), lambda i: (ai(i), 0))]
        + [pl.BlockSpec((d, ft), lambda i: (0, fi(i)))] * 2
        + [pl.BlockSpec((ft, d), lambda i: (fi(i), 0))],
        out_specs=[full((t, d)), full((t, d)), any_, any_],
        out_shape=[jax.ShapeDtypeStruct((t, d), BF), jax.ShapeDtypeStruct((t, d), F32),
                   jax.ShapeDtypeStruct((8, t, d), BF), jax.ShapeDtypeStruct((8, el, t), F32)],
        scratch_shapes=[pltpu.VMEM((t, d), BF), pltpu.VMEM((t, d), F32), pltpu.VMEM((t, d), BF),
                        pltpu.VMEM((ne, t), F32),
                        dma((3,)), dma((3,)), dma((2,)), dma((2,)), dma((3,)), dma((3,)), dma((7,)), dma((7,)), dma((2,))],
        cost_estimate=pl.CostEstimate(flops=8 * t * d * d, bytes_accessed=8 * d * d, transcendentals=0),
        compiler_params=pltpu.CompilerParams(dimension_semantics=("arbitrary",), collective_id=0, has_side_effects=True,
                                             vmem_limit_bytes=56 << 20),
        name="first",
    )(h, na.reshape(1, d), nm.reshape(1, d), nf.reshape(1, d), wr, idx, cos, sin, wq, wk, wv, wo, w1, w3, w2)


def _hid_kernel(off_ref, nb_ref, g_ref, u_hbm, w1_hbm, w3_hbm, hid_hbm, gm_hbm,
                u_sc, x_sc, w1_sc, w3_sc, h_sc, hx_sc, gm_sc, su, sw1, sw3, sh, sg, *, ns, el, cap, nf, mb, depth):
    t, d = u_sc.shape[1:]
    ft = w1_sc.shape[-1]
    rows = ns * cap
    total = el * nf

    def fetch(k):
        slot = lax.rem(k, depth)
        e, f = lax.div(k, nf), lax.rem(k, nf)
        cols = pl.ds(pl.multiple_of(f * ft, ft), ft)
        return (pltpu.make_async_copy(w1_hbm.at[e, :, cols], w1_sc.at[slot], sw1.at[slot]),
                pltpu.make_async_copy(w3_hbm.at[e, :, cols], w3_sc.at[slot], sw3.at[slot]))

    def put_h(k):
        slot = lax.rem(k, 2)
        e, f = lax.div(k, nf), lax.rem(k, nf)
        cols = pl.ds(pl.multiple_of(f * ft, ft), ft)
        return pltpu.make_async_copy(hx_sc.at[slot], hid_hbm.at[e, :, cols], sh.at[slot])

    def put_g(s):
        slot = lax.rem(s, 2)
        return pltpu.make_async_copy(gm_sc.at[slot], gm_hbm.at[s], sg.at[slot])

    def get_u(s):
        return pltpu.make_async_copy(u_hbm.at[s], u_sc.at[s], su.at[s])

    for s in range(ns):
        get_u(s).start()
    for k in range(depth):
        for c in fetch(k):
            c.start()
    h_sc[...] = jnp.zeros_like(h_sc)
    it = lax.broadcasted_iota(jnp.int32, (cap, t), 0).astype(F32)
    before = jnp.where(lax.broadcasted_iota(jnp.int32, (t, t), 0) < lax.broadcasted_iota(jnp.int32, (t, t), 1), 1.0, 0.0)

    @pl.loop(0, ns)
    def _(s):
        g = g_ref[s]
        rank = jnp.where(g >= 0, _dot(jnp.where(g >= 0, 1.0, 0.0), before), -1.0)
        hit = [it == rank[e:e + 1, :] for e in range(el)]
        p = jnp.concatenate([jnp.where(h, 1.0, 0.0).astype(BF) for h in hit], axis=0)
        gt = jnp.concatenate([jnp.where(h, g[e:e + 1, :], 0.0) for e, h in enumerate(hit)], axis=0)
        gm = jnp.transpose(gt)
        ghi = gm.astype(BF)
        r1 = gm - ghi.astype(F32)
        gmid = r1.astype(BF)
        glo = (r1 - gmid.astype(F32)).astype(BF)

        @pl.when(s >= 2)
        def _():
            put_g(s - 2).wait()
        gm_sc[lax.rem(s, 2)] = jnp.concatenate([ghi, gmid, glo], axis=1)
        put_g(s).start()
        get_u(s).wait()
        for c in range(d // 512):
            cs = slice(c * 512, (c + 1) * 512)
            xv = _dot(p, u_sc[s, :, cs]).astype(BF)
            for e in range(el):
                o = pl.multiple_of(off_ref[s * el + e], 16)
                x_sc[e, pl.ds(o, cap), cs] = xv[e * cap:(e + 1) * cap]

    @pl.loop(0, total)
    def _(k):
        slot = lax.rem(k, depth)
        e = lax.div(k, nf)
        for c in fetch(k):
            c.wait()
        for m in range(mb, rows + 1, mb):
            @pl.when(nb_ref[e] == m // mb)
            def _():
                x = x_sc[e, :m, :]
                h1 = _dot(x, w1_sc[slot])
                h3 = _dot(x, w3_sc[slot])
                h_sc[:m, :] = (h1 * jax.nn.sigmoid(h1) * h3).astype(BF)

        @pl.when(k + depth < total)
        def _():
            for c in fetch(k + depth):
                c.start()

        @pl.when(k >= 2)
        def _():
            put_h(k - 2).wait()
        for s in range(ns):
            o = pl.multiple_of(off_ref[s * el + e], 16)
            hx_sc[lax.rem(k, 2), s * cap:(s + 1) * cap, :] = h_sc[pl.ds(o, cap), :]
        put_h(k).start()

    for s in (ns - 2, ns - 1):
        put_g(s).wait()
    for k in (total - 2, total - 1):
        put_h(k).wait()


def _hidden(u_all, g_all, ue1, ue3, cap):
    ns, t, d = u_all.shape
    el, _, fe = ue1.shape
    mb, nf, depth = 128, 2, 4
    ft = fe // nf
    cnt = jnp.sum((g_all >= 0).astype(jnp.int32), axis=-1)
    pad = (cnt + 15) // 16 * 16
    off = jnp.cumsum(pad, axis=0) - pad
    nb = jnp.maximum((jnp.sum(pad, axis=0) + mb - 1) // mb, 1)
    smem, vmem, any_ = (pl.BlockSpec(memory_space=m) for m in (pltpu.SMEM, pltpu.VMEM, pl.ANY))
    dma = pltpu.SemaphoreType.DMA
    return pl.pallas_call(
        functools.partial(_hid_kernel, ns=ns, el=el, cap=cap, nf=nf, mb=mb, depth=depth),
        in_specs=[smem, smem, vmem, any_, any_, any_],
        out_specs=[any_, any_],
        out_shape=[jax.ShapeDtypeStruct((el, ns * cap, fe), BF), jax.ShapeDtypeStruct((ns, t, 3 * el * cap), BF)],
        scratch_shapes=[pltpu.VMEM((ns, t, d), BF), pltpu.VMEM((el, ns * cap, d), BF), pltpu.VMEM((depth, d, ft), BF),
                        pltpu.VMEM((depth, d, ft), BF), pltpu.VMEM((ns * cap, ft), BF), pltpu.VMEM((2, ns * cap, ft), BF),
                        pltpu.VMEM((2, t, 3 * el * cap), BF),
                        dma((ns,)), dma((depth,)), dma((depth,)), dma((2,)), dma((2,))],
        cost_estimate=pl.CostEstimate(flops=4 * el * ns * cap * d * fe, bytes_accessed=4 * el * d * fe, transcendentals=0),
        compiler_params=pltpu.CompilerParams(vmem_limit_bytes=58 << 20),
        name="hidden",
    )(off.reshape(-1), nb, g_all, u_all, ue1, ue3)


E0 = {q: q + 1 for q in range(8)}
E1 = {0: 4, 1: 4, 2: 5, 3: 6, 4: 7, 5: 11, 6: 12, 7: 12}
E2 = {0: 8, 1: 8, 2: 9, 3: 10, 4: 12, 5: 12, 6: 12, 7: 12}
NQ, F_FROM, STEPS = 8, 4, 13


def _last_kernel(hid_hbm, gm_hbm, z_ref, f_ref, ue2_ref, w1_ref, w3_ref, w2_ref, o_ref,
                 hid_sc, gm_sc, y_sc, keep_sc, ps_sc, r0_sc, r1_sc, r2_sc, acc_sc, hs, gs, s0, r0, s1, r1, s2, r2,
                 *, ns, el, cap, nfs):
    i = pl.program_id(0)
    t, d = z_ref.shape
    cw = ue2_ref.shape[-1]
    me = lax.axis_index('ep')

    def get_h(e):
        return pltpu.make_async_copy(hid_hbm.at[e], hid_sc.at[e], hs.at[e])

    def get_g(s):
        return pltpu.make_async_copy(gm_hbm.at[s], gm_sc.at[s], gs.at[s])

    def remote(src, dst, s, r, dev):
        return pltpu.make_async_remote_copy(src_ref=src, dst_ref=dst, send_sem=s, recv_sem=r,
                                            device_id={'ep': dev}, device_id_type=MESH)

    def turn(q, even, odd):
        return even if q % 2 == 0 else odd

    def send0(q, slot):
        return remote(ps_sc.at[slot], r0_sc.at[q], s0.at[q], r0.at[q], _peer(me, 1))

    def send1(q):
        return remote(r0_sc.at[q, pl.ds(2, 2)], r1_sc.at[q], s1.at[q], r1.at[q], _peer(me, turn(q, 2, 4)))

    def send2(q):
        return remote(r0_sc.at[q, 1], r2_sc.at[q], s2.at[q], r2.at[q], _peer(me, turn(q, 4, 2)))

    @pl.when(i == 0)
    def _():
        arrived = _barrier(me, (1, 2, 4))
        for e in range(el):
            get_h(e).start()
        for s in range(ns):
            get_g(s).start()
        acc_sc[...] = f_ref[...]
        arrived()

    @pl.when(i < NQ)
    def _():
        for e in range(el):
            @pl.when(i == 0)
            def _():
                get_h(e).wait()
            y = _dot(hid_sc[e], ue2_ref[e]).astype(BF)
            for s in range(ns):
                y_sc[s, e * cap:(e + 1) * cap, :] = y[s * cap:(s + 1) * cap]

    for q, step in E0.items():
        @pl.when(i == step)
        def _():
            send0(q, q % 2).wait_recv()
            r0_sc[q] += keep_sc[...]
            send1(q).start()

    @pl.when(i == 0)
    def _():
        for s in range(ns):
            get_g(s).wait()

    @pl.when((i >= 2) & (i < NQ))
    def _():
        send0(i - 2, i % 2).wait_send()

    @pl.when(i < NQ)
    def _():
        odd = i % 2
        kk = el * cap
        for b in range(4):
            for c in range(2):
                s = c + (0, 4 - 2 * odd, 2 + 2 * odd, 6)[b]
                y = y_sc[s]
                m = _dot(gm_sc[s, :, :kk], y) + _dot(gm_sc[s, :, kk:2 * kk], y) + _dot(gm_sc[s, :, 2 * kk:], y)
                if c == 0:
                    keep_sc[b] = m
                else:
                    ps_sc[i % 2, b] = m
        send0(i, i % 2).start()

    @pl.when((i >= F_FROM) & (i < F_FROM + nfs))
    def _():
        acc_sc[...] += _ffn_tile(z_ref[...], w1_ref[...], w3_ref[...], w2_ref[...])

    for q, step in E1.items():
        @pl.when(i == step)
        def _():
            send1(q).wait_recv()
            r0_sc[q, 0:2] += r1_sc[q]
            send2(q).start()

    for q, step in E2.items():
        @pl.when(i == step)
        def _():
            send2(q).wait_recv()
            acc_sc[:, q * cw:(q + 1) * cw] += r0_sc[q, 0] + r2_sc[q]

    @pl.when(i == STEPS - 1)
    def _():
        for q in (NQ - 2, NQ - 1):
            send0(q, q % 2).wait_send()
        for q in range(NQ):
            send1(q).wait_send()
            send2(q).wait_send()
        o_ref[...] = acc_sc[...].astype(BF)


def _last(hid, gm, z, f, ue2, w1, w3, w2, cap, ft, f0):
    t, d = z.shape
    el, rows, fe = hid.shape
    ns = rows // cap
    cw = d // NQ
    nfs = w1.shape[1] // ft - f0
    full = lambda shape: pl.BlockSpec(shape, lambda i: (0, 0), pipeline_mode=pl.Buffered(1))
    qi = lambda i: jnp.minimum(i, NQ - 1)
    fi = lambda i: f0 + jnp.clip(i - F_FROM, 0, nfs - 1)
    any_ = pl.BlockSpec(memory_space=pl.ANY)
    dma = pltpu.SemaphoreType.DMA
    return pl.pallas_call(
        functools.partial(_last_kernel, ns=ns, el=el, cap=cap, nfs=nfs),
        grid=(STEPS,),
        in_specs=[any_, any_, full((t, d)), full((t, d)),
                  pl.BlockSpec((el, fe, cw), lambda i: (0, 0, qi(i)))]
        + [pl.BlockSpec((d, ft), lambda i: (0, fi(i)))] * 2
        + [pl.BlockSpec((ft, d), lambda i: (fi(i), 0))],
        out_specs=full((t, d)),
        out_shape=jax.ShapeDtypeStruct((t, d), BF),
        scratch_shapes=[pltpu.VMEM((el, rows, fe), BF), pltpu.VMEM(gm.shape, BF), pltpu.VMEM((ns, el * cap, cw), BF),
                        pltpu.VMEM((4, t, cw), F32), pltpu.VMEM((2, 4, t, cw), F32), pltpu.VMEM((NQ, 4, t, cw), F32),
                        pltpu.VMEM((NQ, 2, t, cw), F32), pltpu.VMEM((NQ, t, cw), F32), pltpu.VMEM((t, d), F32),
                        dma((el,)), dma((ns,))] + [dma((NQ,))] * 6,
        cost_estimate=pl.CostEstimate(flops=2 * el * rows * d * fe, bytes_accessed=2 * el * d * fe, transcendentals=0),
        compiler_params=pltpu.CompilerParams(dimension_semantics=("arbitrary",), collective_id=1, has_side_effects=True,
                                             vmem_limit_bytes=67043328),
        name="last",
    )(hid, gm, z, f, ue2, w1, w3, w2)


def solution(mesh):
    G = mesh.shape['ep']
    ft, f0 = 512, 8

    def local(h0, idx, slot, na, wq, wk, wv, wo, nf, w1, w3, w2, nm, wr, ue1, ue3, ue2):
        b, s, d = h0.shape
        t = b * s
        k = idx.shape[-1]
        el = ue1.shape[0]
        cap = 2 * t * k // (el * G)
        z, f, u_all, g_all = _first(h0.reshape(t, d), na, nm, nf, wr, idx.reshape(t, k), wq, wk, wv, wo, w1, w3, w2,
                                    el, f0, ft)
        hid, gm = _hidden(u_all, g_all, ue1, ue3, cap)
        return _last(hid, gm, z, f, ue2, w1, w3, w2, cap, ft, f0).reshape(b, s, d)

    rows_spec = P(('dp', 'ep'))
    in_specs = (rows_spec,) * 3 + (P(),) * 11 + (P('ep'),) * 3
    return jax.shard_map(local, mesh=mesh, in_specs=in_specs, out_specs=rows_spec, check_vma=False)
```

time: 622 us -> 211 us (0.34); the launches traced: 612 us -> 210 us
  Pallas kernels: 0 us -> 197 us
  blocking collectives: 189 us -> 0 us
  matrix products: 144 us -> 0 us
  local copies, waits for them, and re-layouts: 146 us -> 9.77 us
  waiting for transfers between devices: 98.4 us -> 0 us
  other arithmetic: 27.7 us -> 3.58 us
    pallas_call x0 -> x3, Pallas kernels: none -> 197 us  [the longest x1 102 us: _last(): pl.pallas_call(functools.partial(_last_kernel, ns=ns, el=el, cap=cap, nfs...]
    all_to_all x1 -> x0, blocking collectives: 189 us -> none  [local(): recv = lax.all_to_all(send, 'ep', 0, 0, tiled=True)]
    dot_general x11 -> x0, matrix products: 144 us -> none  [the longest x1 45.4 us: _experts(): jnp.einsum('ecf,efd->ecd', hid, ue2, preferred_element_type=f32)]
    all_to_all x1 -> x0, waiting for transfers between devices: 98.4 us -> none  [local(): back = lax.all_to_all(y, 'ep', 0, 0, tiled=True)]
    gather x6 -> x0, local copies, waits for them, and re-layouts: 88.5 us -> none  [the longest x1 50.4 us: local(): yg = back[ix, sl]]
    dot_general x2 -> x0, local copies, waits for them, and re-layouts: 24.6 us -> none  [the longest x1 12.3 us: _dense(): jnp.dot(x, wk, preferred_element_type=f32).reshape(b, s, nkvv, HEAD)]
    transpose x2 -> x0, local copies, waits for them, and re-layouts: 20.7 us -> none  [the longest x1 14.1 us: local(): y = y.reshape(el, G, cap, d).transpose(1, 0, 2, 3).reshape(e, cap, d)]
    reduce_sum x4 -> x2, other arithmetic: 13.8 us -> 1.08 us  [the longest x1 1.05 us: _hidden(): cnt = jnp.sum((g_all >= 0).astype(jnp.int32), axis=-1)]
  transfers between devices with their start and end apart: 1 -> 0, of which waited for: 1 -> 0; matrix products, arithmetic and copies ran while one was open for 14% -> 0% of each run, Pallas kernels for 0% -> 0%
where the time goes in v2:
time: 211 us; the launch traced here: 210 us
  Pallas kernels  197 us (93%)
  local copies, waits for them, and re-layouts  9.77 us (5%)
  other arithmetic  3.58 us (2%)
    pallas_call x1, Pallas kernels, _last(): pl.pallas_call(functools.partial(_last_kernel, ns=ns, el=el, cap=cap, nfs...  102 us
    pallas_call x1, Pallas kernels, _first(): pl.pallas_call(functools.partial(_first_kernel, na_steps=na_steps, nf_ste...  52.6 us
    pallas_call x1, Pallas kernels, _hidden(): pl.pallas_call(functools.partial(_hid_kernel, ns=ns, el=el, cap=cap, nf=n...  41.9 us
    unnamed x3, local copies, waits for them, and re-layouts  5.74 us

profile of v2, /device:TPU:0, one launch (start us, length us, event | category | flops | bytes accessed | tf_op | source)
XLA Modules:
  0.0 210.3 jit_solution(6404027450042642356)
XLA Ops:
  0.0 1.3 reshape.34.na_ref
  1.3 1.3 reshape.36.nf_ref
  2.6 1.3 reshape.35.nm_ref
  3.9 1.5 copy.17
  5.4 0.5 fusion
  5.9 0.9 pad_maximum_fusion
  6.8 2.0 copy.18.wr_ref
  8.7 52.6 %first.1 = (bf16[256,2048]{1,0:T(8,128)(2,1)}, f32[256,2048]{1,0:T(8,128)}, bf16[8,256,2048]{2,1,0:T(8,128)(2,1)}, f32[8,8,256]{2,1,0:T(8,128)}) custom-call(bf16[256,2048]{1,0:T(8,128)(2,1)} %bitcast.4, bf16[1,2048]{1,0:T(2,128)(2,1)} %reshape.34.na_ref, bf16[1,2048]{1,0:T(2,128)(2,1)} %reshape.35.nm_ref, bf16[1,2048]{1,0:T(2,128)(2,1)} %reshape.36.nf_ref, ...), custom_call_target="tpu_custom_call" | custom-call | flops 8589934592 | bytes 33554432 | tf_op jit(solution)/shard_map/first/pallas_call | solution.py:186
  61.3 1.1 convert_reduce_fusion
  62.4 0.5 fusion.4.nb_ref
  62.9 0.1 add.21
  63.0 0.1 reduce_window_sum.14
  63.1 0.5 multiply_subtract_fusion.off_ref
  63.6 41.9 %hidden.1 = (bf16[8,512,1024]{2,1,0:T(8,128)(2,1)}, bf16[8,256,1536]{2,1,0:T(8,128)(2,1)}) custom-call(s32[64]{0:T(128)} %multiply_subtract_fusion.off_ref, s32[8]{0:T(128)} %fusion.4.nb_ref, f32[8,8,256]{2,1,0:T(8,128)} %get-tuple-element.11.g_ref, bf16[8,256,2048]{2,1,0:T(8,128)(2,1)} %get-tuple-element.12.u_hbm, bf16[8,2048,1024]{2,1,0:T(8,128)(2,1)} %w1_hbm.1, ...), custom_call_target="tpu_custom_call" | custom-call | flops 34359738368 | bytes 67108864 | tf_op jit(solution)/shard_map/hidden/pallas_call | solution.py:315
  105.6 102.4 %last.1 = bf16[256,2048]{1,0:T(8,128)(2,1)} custom-call(bf16[8,512,1024]{2,1,0:T(8,128)(2,1)} %get-tuple-element.13.hid_hbm, bf16[8,256,1536]{2,1,0:T(8,128)(2,1)} %get-tuple-element.14.gm_hbm, bf16[256,2048]{1,0:T(8,128)(2,1)} %get-tuple-element.15.z_ref, f32[256,2048]{1,0:T(8,128)} %get-tuple-element.16.f_ref, bf16[8,1024,2048]{2,1,0:T(8,128)(2,1)} %ue2_ref.1, ...), custom_call_target="tpu_custom_call" | custom-call | flops 17179869184 | bytes 33554432 | tf_op jit(solution)/shard_map/last/pallas_call | solution.py:455
  208.0 2.3 %copy.20 = bf16[1,256,2048]{2,1,0:T(8,128)(2,1)} copy(bf16[1,256,2048]{2,1,0:T(8,128)(2,1)} %bitcast.3) | data formatting | bytes 2097152
  (4 shorter events, 0.1 us)

commit v3 on v2

--- a/solution.py
+++ b/solution.py
@@ -16,7 +16,7 @@
 def _rms(x, w):
     xf = x.astype(F32)
     r = lax.rsqrt(jnp.mean(xf * xf, axis=-1, keepdims=True) + EPS)
-    return (xf * r * w.astype(F32)).astype(BF)
+    return (xf * r * w.astype(F32).reshape(1, -1)).astype(BF)
 
 
 def _dot(a, b):
@@ -44,6 +44,38 @@
     return lambda: pl.semaphore_wait(sem, len(rels))
 
 
+class _Tiles:
+    def __init__(self, hbm, vmem, sems, first, count):
+        self.hbm, self.vmem, self.sems, self.first, self.count = hbm, vmem, sems, first, count
+
+    def copies(self, k):
+        slot = lax.rem(k, 2)
+        ft = self.vmem[0].shape[-1]
+        part = pl.ds(pl.multiple_of((self.first + k) * ft, ft), ft)
+        w1, w3, w2 = self.hbm
+        src = (w1.at[:, part], w3.at[:, part], w2.at[part])
+        return [pltpu.make_async_copy(a, b.at[slot], c.at[slot]) for a, b, c in zip(src, self.vmem, self.sems)]
+
+    def start(self, k):
+        for c in self.copies(k):
+            c.start()
+
+    def add(self, k, z, acc_ref):
+        for c in self.copies(k):
+            c.wait()
+        slot = lax.rem(k, 2)
+        acc_ref[...] += _ffn_tile(z, *(v[slot] for v in self.vmem))
+
+        @pl.when(k + 2 < self.count)
+        def _():
+            self.start(k + 2)
+
+
+def _tile_scratch(d, ft):
+    dma = pltpu.SemaphoreType.DMA
+    return [pltpu.VMEM((2, d, ft), BF), pltpu.VMEM((2, d, ft), BF), pltpu.VMEM((2, ft, d), BF), dma((2,)), dma((2,)), dma((2,))]
+
+
 def _ffn_tile(z, w1, w3, w2):
     h1 = _dot(z, w1)
     h3 = _dot(z, w3)
@@ -52,13 +84,15 @@
 
 
 def _first_kernel(h_ref, na_ref, nm_ref, nf_ref, wr_ref, idx_ref, cos_ref, sin_ref, wq_ref, wk_ref, wv_ref, wo_ref,
-                  w1_ref, w3_ref, w2_ref, z_ref, f_ref, uall_ref, gall_ref,
-                  x_sc, acc_sc, u_sc, g_sc, sa, ra, sb, rb, sc, rc, sg, rg, ls, *, na_steps, nf_steps, hps, el, step_b, step_c):
+                  w1_hbm, w3_hbm, w2_hbm, z_ref, f_ref, uall_ref, gall_ref,
+                  x_sc, acc_sc, u_sc, g_sc, sa, ra, sb, rb, sc, rc, sg, rg, ls, t1, t3, t2, q1, q3, q2s,
+                  *, na_steps, nf_steps, hps, el, step_b, step_c):
     i = pl.program_id(0)
     t, d = h_ref.shape
     me = lax.axis_index('ep')
     hops = (1, 2, 4)
     half = t // 2
+    tiles = _Tiles((w1_hbm, w3_hbm, w2_hbm), (t1, t3, t2), (q1, q3, q2s), 0, nf_steps)
 
     def remote(src, dst, s, r, rel):
         return pltpu.make_async_remote_copy(src_ref=src, dst_ref=dst, send_sem=s, recv_sem=r,
@@ -88,16 +122,14 @@
         arrived = _barrier(me, range(1, 8))
         u = _rms(h_ref[...], nm_ref[...])
         u_sc[...] = u
-        logits = _dot(u, wr_ref[...])
-        ne = logits.shape[1]
-        lane = lax.broadcasted_iota(jnp.int32, (t, ne), 1)
-        routed = lane == idx_ref[:, 0:1]
-        for j in range(1, idx_ref.shape[1]):
-            routed = routed | (lane == idx_ref[:, j:j + 1])
+        logits = lax.dot_general(wr_ref[...], u, (((1,), (1,)), ((), ())), preferred_element_type=F32)
+        row = lax.broadcasted_iota(jnp.int32, logits.shape, 0)
+        routed = row == idx_ref[0:1, :]
+        for j in range(1, idx_ref.shape[0]):
+            routed = routed | (row == idx_ref[j:j + 1, :])
         lg = jnp.where(routed, logits, -jnp.inf)
-        ex = jnp.exp(lg - jnp.max(lg, axis=-1, keepdims=True))
-        g = jnp.where(routed, ex / jnp.sum(ex, axis=-1, keepdims=True), -1.0)
-        g_sc[...] = jnp.transpose(jnp.concatenate([g] * (128 // ne), axis=1))[:ne]
+        ex = jnp.exp(lg - jnp.max(lg, axis=0, keepdims=True))
+        g_sc[...] = jnp.where(routed, ex / jnp.sum(ex, axis=0, keepdims=True), -1.0)
         arrived()
         for n in (1, 2, 0):
             stage_a(n).start()
@@ -148,11 +180,16 @@
             stage_b(n).wait_recv()
         stage_c(2).start()
 
-    @pl.when(i >= na_steps)
-    def _():
-        f_ref[...] += _ffn_tile(z_ref[...], w1_ref[...], w3_ref[...], w2_ref[...])
-
-    @pl.when(i == na_steps + nf_steps - 1)
+    @pl.when(i == na_steps - 3)
+    def _():
+        tiles.start(0)
+        tiles.start(1)
+
+    @pl.when((i >= na_steps) & (i < na_steps + nf_steps))
+    def _():
+        tiles.add(i - na_steps, z_ref[...], f_ref)
+
+    @pl.when(i == na_steps + nf_steps)
     def _():
         stage_a(0).wait_recv()
         for n in range(3):
@@ -172,38 +209,37 @@
     hps = 2
     w = HEAD * hps
     na_steps = wq.shape[1] // w
-    ne = wr.shape[1]
+    ne = wr.shape[0]
     pos = jnp.arange(t).astype(F32)
     inv = ROPE_BASE ** (-2.0 * jnp.arange(HEAD // 2).astype(F32) / HEAD)
     ang = pos[:, None] * inv[None, :]
     c, s = jnp.cos(ang), jnp.sin(ang)
     cos, sin = jnp.concatenate([c, c], 1), jnp.concatenate([-s, s], 1)
     full = lambda shape: pl.BlockSpec(shape, lambda i: (0, 0))
+    vec = pl.BlockSpec((d,), lambda i: (0,))
     ai = lambda i: jnp.minimum(i, na_steps - 1)
-    fi = lambda i: jnp.maximum(i - na_steps, 0)
     any_ = pl.BlockSpec(memory_space=pl.ANY)
     dma = pltpu.SemaphoreType.DMA
     return pl.pallas_call(
-        functools.partial(_first_kernel, na_steps=na_steps, nf_steps=nf_steps, hps=hps, el=el, step_b=na_steps + 1,
-                          step_c=na_steps + nf_steps - 2),
-        grid=(na_steps + nf_steps,),
-        in_specs=[full((t, d)), full((1, d)), full((1, d)), full((1, d)), full((d, ne)), full(idx.shape),
+        functools.partial(_first_kernel, na_steps=na_steps, nf_steps=nf_steps, hps=hps, el=el, step_b=na_steps,
+                          step_c=na_steps + nf_steps),
+        grid=(na_steps + nf_steps + 1,),
+        in_specs=[full((t, d)), vec, vec, vec, full((ne, d)), full(idx.shape),
                   full((t, HEAD)), full((t, HEAD))]
         + [pl.BlockSpec((d, w), lambda i: (0, ai(i)))] * 3
         + [pl.BlockSpec((w, d), lambda i: (ai(i), 0))]
-        + [pl.BlockSpec((d, ft), lambda i: (0, fi(i)))] * 2
-        + [pl.BlockSpec((ft, d), lambda i: (fi(i), 0))],
+        + [any_] * 3,
         out_specs=[full((t, d)), full((t, d)), any_, any_],
         out_shape=[jax.ShapeDtypeStruct((t, d), BF), jax.ShapeDtypeStruct((t, d), F32),
                    jax.ShapeDtypeStruct((8, t, d), BF), jax.ShapeDtypeStruct((8, el, t), F32)],
         scratch_shapes=[pltpu.VMEM((t, d), BF), pltpu.VMEM((t, d), F32), pltpu.VMEM((t, d), BF),
                         pltpu.VMEM((ne, t), F32),
-                        dma((3,)), dma((3,)), dma((2,)), dma((2,)), dma((3,)), dma((3,)), dma((7,)), dma((7,)), dma((2,))],
+                        dma((3,)), dma((3,)), dma((2,)), dma((2,)), dma((3,)), dma((3,)), dma((7,)), dma((7,)), dma((2,))] + _tile_scratch(d, ft),
         cost_estimate=pl.CostEstimate(flops=8 * t * d * d, bytes_accessed=8 * d * d, transcendentals=0),
         compiler_params=pltpu.CompilerParams(dimension_semantics=("arbitrary",), collective_id=0, has_side_effects=True,
                                              vmem_limit_bytes=56 << 20),
         name="first",
-    )(h, na.reshape(1, d), nm.reshape(1, d), nf.reshape(1, d), wr, idx, cos, sin, wq, wk, wv, wo, w1, w3, w2)
+    )(h, na, nm, nf, wr, idx, cos, sin, wq, wk, wv, wo, w1, w3, w2)
 
 
 def _hid_kernel(off_ref, nb_ref, g_ref, u_hbm, w1_hbm, w3_hbm, hid_hbm, gm_hbm,
@@ -328,18 +364,19 @@
 
 
 E0 = {q: q + 1 for q in range(8)}
-E1 = {0: 4, 1: 4, 2: 5, 3: 6, 4: 7, 5: 11, 6: 12, 7: 12}
-E2 = {0: 8, 1: 8, 2: 9, 3: 10, 4: 12, 5: 12, 6: 12, 7: 12}
-NQ, F_FROM, STEPS = 8, 4, 13
-
-
-def _last_kernel(hid_hbm, gm_hbm, z_ref, f_ref, ue2_ref, w1_ref, w3_ref, w2_ref, o_ref,
+E1 = {0: 4, 1: 4, 2: 5, 3: 6, 4: 8, 5: 10, 6: 14, 7: 16}
+E2 = {0: 8, 1: 8, 2: 12, 3: 12, 4: 15, 5: 16, 6: 16, 7: 16}
+NQ, F_FROM, STEPS = 8, 4, 17
+
+
+def _last_kernel(hid_hbm, gm_hbm, z_ref, f_ref, ue2_ref, w1_hbm, w3_hbm, w2_hbm, o_ref,
                  hid_sc, gm_sc, y_sc, keep_sc, ps_sc, r0_sc, r1_sc, r2_sc, acc_sc, hs, gs, s0, r0, s1, r1, s2, r2,
-                 *, ns, el, cap, nfs):
+                 t1, t3, t2, q1, q3, q2s, *, ns, el, cap, f0, nfs):
     i = pl.program_id(0)
     t, d = z_ref.shape
     cw = ue2_ref.shape[-1]
     me = lax.axis_index('ep')
+    tiles = _Tiles((w1_hbm, w3_hbm, w2_hbm), (t1, t3, t2), (q1, q3, q2s), f0, nfs)
 
     def get_h(e):
         return pltpu.make_async_copy(hid_hbm.at[e], hid_sc.at[e], hs.at[e])
@@ -372,28 +409,34 @@
             get_g(s).start()
         acc_sc[...] = f_ref[...]
         arrived()
+        for e in range(el):
+            get_h(e).wait()
+
+    def pass_on(qs):
+        for q in qs:
+            @pl.when(i == E0[q])
+            def _():
+                send0(q, q % 2).wait_recv()
+                r0_sc[q] += keep_sc[...]
+                send1(q).start()
+
+    pass_on((0, 1))
 
     @pl.when(i < NQ)
     def _():
         for e in range(el):
-            @pl.when(i == 0)
-            def _():
-                get_h(e).wait()
             y = _dot(hid_sc[e], ue2_ref[e]).astype(BF)
             for s in range(ns):
                 y_sc[s, e * cap:(e + 1) * cap, :] = y[s * cap:(s + 1) * cap]
 
-    for q, step in E0.items():
-        @pl.when(i == step)
-        def _():
-            send0(q, q % 2).wait_recv()
-            r0_sc[q] += keep_sc[...]
-            send1(q).start()
+    pass_on(range(2, NQ))
 
     @pl.when(i == 0)
     def _():
         for s in range(ns):
             get_g(s).wait()
+        tiles.start(0)
+        tiles.start(1)
 
     @pl.when((i >= 2) & (i < NQ))
     def _():
@@ -416,7 +459,7 @@
 
     @pl.when((i >= F_FROM) & (i < F_FROM + nfs))
     def _():
-        acc_sc[...] += _ffn_tile(z_ref[...], w1_ref[...], w3_ref[...], w2_ref[...])
+        tiles.add(i - F_FROM, z_ref[...], acc_sc)
 
     for q, step in E1.items():
         @pl.when(i == step)
@@ -449,22 +492,19 @@
     nfs = w1.shape[1] // ft - f0
     full = lambda shape: pl.BlockSpec(shape, lambda i: (0, 0), pipeline_mode=pl.Buffered(1))
     qi = lambda i: jnp.minimum(i, NQ - 1)
-    fi = lambda i: f0 + jnp.clip(i - F_FROM, 0, nfs - 1)
     any_ = pl.BlockSpec(memory_space=pl.ANY)
     dma = pltpu.SemaphoreType.DMA
     return pl.pallas_call(
-        functools.partial(_last_kernel, ns=ns, el=el, cap=cap, nfs=nfs),
+        functools.partial(_last_kernel, ns=ns, el=el, cap=cap, f0=f0, nfs=nfs),
         grid=(STEPS,),
         in_specs=[any_, any_, full((t, d)), full((t, d)),
-                  pl.BlockSpec((el, fe, cw), lambda i: (0, 0, qi(i)))]
-        + [pl.BlockSpec((d, ft), lambda i: (0, fi(i)))] * 2
-        + [pl.BlockSpec((ft, d), lambda i: (fi(i), 0))],
+                  pl.BlockSpec((el, fe, cw), lambda i: (0, 0, qi(i)))] + [any_] * 3,
         out_specs=full((t, d)),
         out_shape=jax.ShapeDtypeStruct((t, d), BF),
         scratch_shapes=[pltpu.VMEM((el, rows, fe), BF), pltpu.VMEM(gm.shape, BF), pltpu.VMEM((ns, el * cap, cw), BF),
                         pltpu.VMEM((4, t, cw), F32), pltpu.VMEM((2, 4, t, cw), F32), pltpu.VMEM((NQ, 4, t, cw), F32),
                         pltpu.VMEM((NQ, 2, t, cw), F32), pltpu.VMEM((NQ, t, cw), F32), pltpu.VMEM((t, d), F32),
-                        dma((el,)), dma((ns,))] + [dma((NQ,))] * 6,
+                        dma((el,)), dma((ns,))] + [dma((NQ,))] * 6 + _tile_scratch(d, ft),
         cost_estimate=pl.CostEstimate(flops=2 * el * rows * d * fe, bytes_accessed=2 * el * d * fe, transcendentals=0),
         compiler_params=pltpu.CompilerParams(dimension_semantics=("arbitrary",), collective_id=1, has_side_effects=True,
                                              vmem_limit_bytes=67043328),
@@ -474,7 +514,7 @@
 
 def solution(mesh):
     G = mesh.shape['ep']
-    ft, f0 = 512, 8
+    ft, f0 = 512, 4
 
     def local(h0, idx, slot, na, wq, wk, wv, wo, nf, w1, w3, w2, nm, wr, ue1, ue3, ue2):
         b, s, d = h0.shape
@@ -482,7 +522,7 @@
         k = idx.shape[-1]
         el = ue1.shape[0]
         cap = 2 * t * k // (el * G)
-        z, f, u_all, g_all = _first(h0.reshape(t, d), na, nm, nf, wr, idx.reshape(t, k), wq, wk, wv, wo, w1, w3, w2,
+        z, f, u_all, g_all = _first(h0.reshape(t, d), na, nm, nf, wr.T, idx.reshape(t, k).T, wq, wk, wv, wo, w1, w3, w2,
                                     el, f0, ft)
         hid, gm = _hidden(u_all, g_all, ue1, ue3, cap)
         return _last(hid, gm, z, f, ue2, w1, w3, w2, cap, ft, f0).reshape(b, s, d)

time: 211 us -> 191 us (0.905)
  Pallas kernels: 197 us -> 183 us
  local copies, waits for them, and re-layouts: 9.77 us -> 2.46 us
    pallas_call x1, Pallas kernels: 102 us -> 91.9 us  [_last(): pl.pallas_call(functools.partial(_last_kernel, ns=ns, el=el, cap=cap, f0=...]
    reshape x3 -> x0, local copies, waits for them, and re-layouts: 3.87 us -> none  [the longest x1 1.29 us: _first(): na.reshape(1, d)]
    pallas_call x1, Pallas kernels: 52.6 us -> 48.7 us  [_first(): pl.pallas_call(functools.partial(_first_kernel, na_steps=na_steps, nf_ste...]
    unnamed x3 -> x1, local copies, waits for them, and re-layouts: 5.74 us -> 2.3 us
where the time goes in v3:
time: 191 us; the launch traced here: 189 us
  Pallas kernels  183 us (96%)
  other arithmetic  3.56 us (2%)
  local copies, waits for them, and re-layouts  2.46 us (1%)
    pallas_call x1, Pallas kernels, _last(): pl.pallas_call(functools.partial(_last_kernel, ns=ns, el=el, cap=cap, f0=...  91.9 us
    pallas_call x1, Pallas kernels, _first(): pl.pallas_call(functools.partial(_first_kernel, na_steps=na_steps, nf_ste...  48.7 us
    pallas_call x1, Pallas kernels, _hidden(): pl.pallas_call(functools.partial(_hid_kernel, ns=ns, el=el, cap=cap, nf=n...  41.9 us

profile of v3, /device:TPU:0, one launch (start us, length us, event | category | flops | bytes accessed | tf_op | source)
XLA Modules:
  0.0 188.6 jit_solution(18291237810615277383)
XLA Ops:
  0.0 0.5 fusion
  0.6 0.8 pad_maximum_fusion
  1.4 48.7 %first.1 = (bf16[256,2048]{1,0:T(8,128)(2,1)}, f32[256,2048]{1,0:T(8,128)}, bf16[8,256,2048]{2,1,0:T(8,128)(2,1)}, f32[8,8,256]{2,1,0:T(8,128)}) custom-call(bf16[256,2048]{1,0:T(8,128)(2,1)} %bitcast.7, bf16[2048]{0:T(1024)(128)(2,1)} %na_ref.1, bf16[2048]{0:T(1024)(128)(2,1)} %nm_ref.1, bf16[2048]{0:T(1024)(128)(2,1)} %nf_ref.1, bf16[64,2048]{1,0:T(8,128)(2,1)} %bitcast.8, ...), custom_call_target="tpu_custom_call" | custom-call | flops 8589934592 | bytes 33554432 | tf_op jit(solution)/shard_map/first/pallas_call | solution.py:223
  50.1 1.1 convert_reduce_fusion
  51.2 0.5 fusion.4.nb_ref
  51.7 0.1 add.21
  51.8 0.1 reduce_window_sum.14
  51.9 0.5 multiply_subtract_fusion.off_ref
  52.5 41.9 %hidden.1 = (bf16[8,512,1024]{2,1,0:T(8,128)(2,1)}, bf16[8,256,1536]{2,1,0:T(8,128)(2,1)}) custom-call(s32[64]{0:T(128)} %multiply_subtract_fusion.off_ref, s32[8]{0:T(128)} %fusion.4.nb_ref, f32[8,8,256]{2,1,0:T(8,128)} %get-tuple-element.11.g_ref, bf16[8,256,2048]{2,1,0:T(8,128)(2,1)} %get-tuple-element.12.u_hbm, bf16[8,2048,1024]{2,1,0:T(8,128)(2,1)} %w1_hbm.4, ...), custom_call_target="tpu_custom_call" | custom-call | flops 34359738368 | bytes 67108864 | tf_op jit(solution)/shard_map/hidden/pallas_call | solution.py:351
  94.4 91.9 %last.1 = bf16[256,2048]{1,0:T(8,128)(2,1)} custom-call(bf16[8,512,1024]{2,1,0:T(8,128)(2,1)} %get-tuple-element.13.hid_hbm, bf16[8,256,1536]{2,1,0:T(8,128)(2,1)} %get-tuple-element.14.gm_hbm, bf16[256,2048]{1,0:T(8,128)(2,1)} %get-tuple-element.15.z_ref, f32[256,2048]{1,0:T(8,128)} %get-tuple-element.16.f_ref, bf16[8,1024,2048]{2,1,0:T(8,128)(2,1)} %ue2_ref.1, ...), custom_call_target="tpu_custom_call" | custom-call | flops 17179869184 | bytes 33554432 | tf_op jit(solution)/shard_map/last/pallas_call | solution.py:497
  186.3 2.3 %copy.18 = bf16[1,256,2048]{2,1,0:T(8,128)(2,1)} copy(bf16[1,256,2048]{2,1,0:T(8,128)(2,1)} %bitcast.6) | data formatting | bytes 2097152
  (4 shorter events, 0.1 us)

commit v4 on v3

--- a/solution.py
+++ b/solution.py
@@ -98,8 +98,12 @@
         return pltpu.make_async_remote_copy(src_ref=src, dst_ref=dst, send_sem=s, recv_sem=r,
                                             device_id={'ep': _peer(me, rel)}, device_id_type=MESH)
 
+    sends_a = ((1, 0, t), (2, 0, half), (4, half, half), (2, half, half), (4, 0, half))
+
     def stage_a(n):
-        return remote(u_sc, uall_ref.at[hops[n]], sa.at[n], ra.at[n], hops[n])
+        rel, start, size = sends_a[n]
+        rows = pl.ds(start, size)
+        return remote(u_sc.at[rows], uall_ref.at[rel, rows], sa.at[n], ra.at[n], rel)
 
     def stage_g(r):
         rows = pl.ds(pl.multiple_of(_peer(me, r) * el, el), el)
@@ -131,7 +135,7 @@
         ex = jnp.exp(lg - jnp.max(lg, axis=0, keepdims=True))
         g_sc[...] = jnp.where(routed, ex / jnp.sum(ex, axis=0, keepdims=True), -1.0)
         arrived()
-        for n in (1, 2, 0):
+        for n in (1, 2, 3, 4, 0):
             stage_a(n).start()
         for r in range(1, 8):
             stage_g(r).start()
@@ -172,6 +176,11 @@
         for n in range(2):
             stage_a(n + 1).wait_recv()
             stage_b(n).start()
+
+    @pl.when(i == na_steps)
+    def _():
+        for n in range(2):
+            stage_a(n + 3).wait_recv()
             stage_c(n).start()
 
     @pl.when(i == step_c)
@@ -192,7 +201,7 @@
     @pl.when(i == na_steps + nf_steps)
     def _():
         stage_a(0).wait_recv()
-        for n in range(3):
+        for n in range(5):
             stage_a(n).wait_send()
         for n in range(2):
             stage_b(n).wait_send()
@@ -221,7 +230,7 @@
     any_ = pl.BlockSpec(memory_space=pl.ANY)
     dma = pltpu.SemaphoreType.DMA
     return pl.pallas_call(
-        functools.partial(_first_kernel, na_steps=na_steps, nf_steps=nf_steps, hps=hps, el=el, step_b=na_steps,
+        functools.partial(_first_kernel, na_steps=na_steps, nf_steps=nf_steps, hps=hps, el=el, step_b=na_steps - 2,
                           step_c=na_steps + nf_steps),
         grid=(na_steps + nf_steps + 1,),
         in_specs=[full((t, d)), vec, vec, vec, full((ne, d)), full(idx.shape),
@@ -234,7 +243,7 @@
                    jax.ShapeDtypeStruct((8, t, d), BF), jax.ShapeDtypeStruct((8, el, t), F32)],
         scratch_shapes=[pltpu.VMEM((t, d), BF), pltpu.VMEM((t, d), F32), pltpu.VMEM((t, d), BF),
                         pltpu.VMEM((ne, t), F32),
-                        dma((3,)), dma((3,)), dma((2,)), dma((2,)), dma((3,)), dma((3,)), dma((7,)), dma((7,)), dma((2,))] + _tile_scratch(d, ft),
+                        dma((5,)), dma((5,)), dma((2,)), dma((2,)), dma((3,)), dma((3,)), dma((7,)), dma((7,)), dma((2,))] + _tile_scratch(d, ft),
         cost_estimate=pl.CostEstimate(flops=8 * t * d * d, bytes_accessed=8 * d * d, transcendentals=0),
         compiler_params=pltpu.CompilerParams(dimension_semantics=("arbitrary",), collective_id=0, has_side_effects=True,
                                              vmem_limit_bytes=56 << 20),
@@ -364,16 +373,17 @@
 
 
 E0 = {q: q + 1 for q in range(8)}
-E1 = {0: 4, 1: 4, 2: 5, 3: 6, 4: 8, 5: 10, 6: 14, 7: 16}
-E2 = {0: 8, 1: 8, 2: 12, 3: 12, 4: 15, 5: 16, 6: 16, 7: 16}
+E1 = {0: 2, 1: 3, 2: 5, 3: 6, 4: 7, 5: 9, 6: 12, 7: 15}
+E2 = {0: 8, 1: 8, 2: 11, 3: 12, 4: 14, 5: 16, 6: 16, 7: 16}
 NQ, F_FROM, STEPS = 8, 4, 17
 
 
-def _last_kernel(hid_hbm, gm_hbm, z_ref, f_ref, ue2_ref, w1_hbm, w3_hbm, w2_hbm, o_ref,
-                 hid_sc, gm_sc, y_sc, keep_sc, ps_sc, r0_sc, r1_sc, r2_sc, acc_sc, hs, gs, s0, r0, s1, r1, s2, r2,
+def _last_kernel(hid_hbm, gm_hbm, z_hbm, f_hbm, ue2_ref, w1_hbm, w3_hbm, w2_hbm, o_ref,
+                 hid_sc, gm_sc, z_ref, y_sc, keep_sc, ps_sc, r0_sc, r1_sc, r2_sc, acc_sc, hs, gs, zs, s0, r0, s1, r1, s2, r2,
                  t1, t3, t2, q1, q3, q2s, *, ns, el, cap, f0, nfs):
     i = pl.program_id(0)
     t, d = z_ref.shape
+    half = t // 2
     cw = ue2_ref.shape[-1]
     me = lax.axis_index('ep')
     tiles = _Tiles((w1_hbm, w3_hbm, w2_hbm), (t1, t3, t2), (q1, q3, q2s), f0, nfs)
@@ -388,17 +398,17 @@
         return pltpu.make_async_remote_copy(src_ref=src, dst_ref=dst, send_sem=s, recv_sem=r,
                                             device_id={'ep': dev}, device_id_type=MESH)
 
-    def turn(q, even, odd):
-        return even if q % 2 == 0 else odd
+    def get_zf():
+        return (pltpu.make_async_copy(z_hbm, z_ref, zs.at[0]), pltpu.make_async_copy(f_hbm, acc_sc, zs.at[1]))
 
     def send0(q, slot):
         return remote(ps_sc.at[slot], r0_sc.at[q], s0.at[q], r0.at[q], _peer(me, 1))
 
-    def send1(q):
-        return remote(r0_sc.at[q, pl.ds(2, 2)], r1_sc.at[q], s1.at[q], r1.at[q], _peer(me, turn(q, 2, 4)))
-
-    def send2(q):
-        return remote(r0_sc.at[q, 1], r2_sc.at[q], s2.at[q], r2.at[q], _peer(me, turn(q, 4, 2)))
+    def send1(q, h):
+        return remote(r0_sc.at[q, h, pl.ds(2, 2)], r1_sc.at[q, h], s1.at[2 * q + h], r1.at[2 * q + h], _peer(me, (2, 4)[h]))
+
+    def send2(q, h):
+        return remote(r0_sc.at[q, h, 1], r2_sc.at[q, h], s2.at[2 * q + h], r2.at[2 * q + h], _peer(me, (4, 2)[h]))
 
     @pl.when(i == 0)
     def _():
@@ -407,7 +417,8 @@
             get_h(e).start()
         for s in range(ns):
             get_g(s).start()
-        acc_sc[...] = f_ref[...]
+        for c in get_zf():
+            c.start()
         arrived()
         for e in range(el):
             get_h(e).wait()
@@ -418,7 +429,8 @@
             def _():
                 send0(q, q % 2).wait_recv()
                 r0_sc[q] += keep_sc[...]
-                send1(q).start()
+                for h in range(2):
+                    send1(q, h).start()
 
     pass_on((0, 1))
 
@@ -444,18 +456,24 @@
 
     @pl.when(i < NQ)
     def _():
-        odd = i % 2
         kk = el * cap
         for b in range(4):
             for c in range(2):
-                s = c + (0, 4 - 2 * odd, 2 + 2 * odd, 6)[b]
+                s = 2 * b + c
                 y = y_sc[s]
                 m = _dot(gm_sc[s, :, :kk], y) + _dot(gm_sc[s, :, kk:2 * kk], y) + _dot(gm_sc[s, :, 2 * kk:], y)
-                if c == 0:
-                    keep_sc[b] = m
-                else:
-                    ps_sc[i % 2, b] = m
+                for h, pos in enumerate(((0, 2, 1, 3)[b], b)):
+                    part = m[h * half:(h + 1) * half]
+                    if c == 0:
+                        keep_sc[h, pos] = part
+                    else:
+                        ps_sc[i % 2, h, pos] = part
         send0(i, i % 2).start()
+
+    @pl.when(i == F_FROM)
+    def _():
+        for c in get_zf():
+            c.wait()
 
     @pl.when((i >= F_FROM) & (i < F_FROM + nfs))
     def _():
@@ -464,23 +482,26 @@
     for q, step in E1.items():
         @pl.when(i == step)
         def _():
-            send1(q).wait_recv()
-            r0_sc[q, 0:2] += r1_sc[q]
-            send2(q).start()
+            for h in range(2):
+                send1(q, h).wait_recv()
+                r0_sc[q, h, 0:2] += r1_sc[q, h]
+                send2(q, h).start()
 
     for q, step in E2.items():
         @pl.when(i == step)
         def _():
-            send2(q).wait_recv()
-            acc_sc[:, q * cw:(q + 1) * cw] += r0_sc[q, 0] + r2_sc[q]
+            for h in range(2):
+                send2(q, h).wait_recv()
+                acc_sc[h * half:(h + 1) * half, q * cw:(q + 1) * cw] += r0_sc[q, h, 0] + r2_sc[q, h]
 
     @pl.when(i == STEPS - 1)
     def _():
         for q in (NQ - 2, NQ - 1):
             send0(q, q % 2).wait_send()
         for q in range(NQ):
-            send1(q).wait_send()
-            send2(q).wait_send()
+            for h in range(2):
+                send1(q, h).wait_send()
+                send2(q, h).wait_send()
         o_ref[...] = acc_sc[...].astype(BF)
 
 
@@ -497,14 +518,16 @@
     return pl.pallas_call(
         functools.partial(_last_kernel, ns=ns, el=el, cap=cap, f0=f0, nfs=nfs),
         grid=(STEPS,),
-        in_specs=[any_, any_, full((t, d)), full((t, d)),
+        in_specs=[any_, any_, any_, any_,
                   pl.BlockSpec((el, fe, cw), lambda i: (0, 0, qi(i)))] + [any_] * 3,
         out_specs=full((t, d)),
         out_shape=jax.ShapeDtypeStruct((t, d), BF),
-        scratch_shapes=[pltpu.VMEM((el, rows, fe), BF), pltpu.VMEM(gm.shape, BF), pltpu.VMEM((ns, el * cap, cw), BF),
-                        pltpu.VMEM((4, t, cw), F32), pltpu.VMEM((2, 4, t, cw), F32), pltpu.VMEM((NQ, 4, t, cw), F32),
-                        pltpu.VMEM((NQ, 2, t, cw), F32), pltpu.VMEM((NQ, t, cw), F32), pltpu.VMEM((t, d), F32),
-                        dma((el,)), dma((ns,))] + [dma((NQ,))] * 6 + _tile_scratch(d, ft),
+        scratch_shapes=[pltpu.VMEM((el, rows, fe), BF), pltpu.VMEM(gm.shape, BF), pltpu.VMEM((t, d), BF),
+                        pltpu.VMEM((ns, el * cap, cw), BF),
+                        pltpu.VMEM((2, 4, t // 2, cw), F32), pltpu.VMEM((2, 2, 4, t // 2, cw), F32),
+                        pltpu.VMEM((NQ, 2, 4, t // 2, cw), F32), pltpu.VMEM((NQ, 2, 2, t // 2, cw), F32),
+                        pltpu.VMEM((NQ, 2, t // 2, cw), F32), pltpu.VMEM((t, d), F32),
+                        dma((el,)), dma((ns,)), dma((2,))] + [dma((NQ,))] * 2 + [dma((2 * NQ,))] * 4 + _tile_scratch(d, ft),
         cost_estimate=pl.CostEstimate(flops=2 * el * rows * d * fe, bytes_accessed=2 * el * d * fe, transcendentals=0),
         compiler_params=pltpu.CompilerParams(dimension_semantics=("arbitrary",), collective_id=1, has_side_effects=True,
                                              vmem_limit_bytes=67043328),

time: 191 us -> 184 us (0.963)
  Pallas kernels: 183 us -> 177 us
    pallas_call x1, Pallas kernels: 91.9 us -> 88 us  [_last(): pl.pallas_call(functools.partial(_last_kernel, ns=ns, el=el, cap=cap, f0=...]
where the time goes in v4:
time: 184 us; the launch traced here: 183 us
  Pallas kernels  177 us (96%)
  other arithmetic  3.56 us (2%)
  local copies, waits for them, and re-layouts  2.46 us (1%)
    pallas_call x1, Pallas kernels, _last(): pl.pallas_call(functools.partial(_last_kernel, ns=ns, el=el, cap=cap, f0=...  88 us
    pallas_call x1, Pallas kernels, _first(): pl.pallas_call(functools.partial(_first_kernel, na_steps=na_steps, nf_ste...  47.5 us
    pallas_call x1, Pallas kernels, _hidden(): pl.pallas_call(functools.partial(_hid_kernel, ns=ns, el=el, cap=cap, nf=n...  41.9 us

profile of v4, /device:TPU:0, one launch (start us, length us, event | category | flops | bytes accessed | tf_op | source)
XLA Modules:
  0.0 183.5 jit_solution(17642246395668922401)
XLA Ops:
  0.0 0.5 fusion
  0.6 0.8 pad_maximum_fusion
  1.4 47.5 %first.1 = (bf16[256,2048]{1,0:T(8,128)(2,1)}, f32[256,2048]{1,0:T(8,128)}, bf16[8,256,2048]{2,1,0:T(8,128)(2,1)}, f32[8,8,256]{2,1,0:T(8,128)}) custom-call(bf16[256,2048]{1,0:T(8,128)(2,1)} %bitcast.7, bf16[2048]{0:T(1024)(128)(2,1)} %na_ref.1, bf16[2048]{0:T(1024)(128)(2,1)} %nm_ref.1, bf16[2048]{0:T(1024)(128)(2,1)} %nf_ref.1, bf16[64,2048]{1,0:T(8,128)(2,1)} %bitcast.8, ...), custom_call_target="tpu_custom_call" | custom-call | flops 8589934592 | bytes 33554432 | tf_op jit(solution)/shard_map/first/pallas_call | solution.py:232
  48.9 1.1 convert_reduce_fusion
  50.0 0.5 fusion.4.nb_ref
  50.5 0.1 add.21
  50.6 0.1 reduce_window_sum.14
  50.7 0.5 multiply_subtract_fusion.off_ref
  51.2 41.9 %hidden.1 = (bf16[8,512,1024]{2,1,0:T(8,128)(2,1)}, bf16[8,256,1536]{2,1,0:T(8,128)(2,1)}) custom-call(s32[64]{0:T(128)} %multiply_subtract_fusion.off_ref, s32[8]{0:T(128)} %fusion.4.nb_ref, f32[8,8,256]{2,1,0:T(8,128)} %get-tuple-element.11.g_ref, bf16[8,256,2048]{2,1,0:T(8,128)(2,1)} %get-tuple-element.12.u_hbm, bf16[8,2048,1024]{2,1,0:T(8,128)(2,1)} %w1_hbm.4, ...), custom_call_target="tpu_custom_call" | custom-call | flops 34359738368 | bytes 67108864 | tf_op jit(solution)/shard_map/hidden/pallas_call | solution.py:360
  93.2 88.0 %last.1 = bf16[256,2048]{1,0:T(8,128)(2,1)} custom-call(bf16[8,512,1024]{2,1,0:T(8,128)(2,1)} %get-tuple-element.13.hid_hbm, bf16[8,256,1536]{2,1,0:T(8,128)(2,1)} %get-tuple-element.14.gm_hbm, bf16[256,2048]{1,0:T(8,128)(2,1)} %get-tuple-element.15.z_hbm, f32[256,2048]{1,0:T(8,128)} %get-tuple-element.16.f_hbm, bf16[8,1024,2048]{2,1,0:T(8,128)(2,1)} %ue2_ref.1, ...), custom_call_target="tpu_custom_call" | custom-call | flops 17179869184 | bytes 33554432 | tf_op jit(solution)/shard_map/last/pallas_call | solution.py:518
  181.2 2.3 %copy.18 = bf16[1,256,2048]{2,1,0:T(8,128)(2,1)} copy(bf16[1,256,2048]{2,1,0:T(8,128)(2,1)} %bitcast.6) | data formatting | bytes 2097152
  (4 shorter events, 0.1 us)

commit v5 on v4

--- a/solution.py
+++ b/solution.py
@@ -24,6 +24,7 @@
 
 
 MESH = pl.DeviceIdType.MESH
+MB = 128
 
 
 def _peer(me, r):
@@ -84,8 +85,8 @@
 
 
 def _first_kernel(h_ref, na_ref, nm_ref, nf_ref, wr_ref, idx_ref, cos_ref, sin_ref, wq_ref, wk_ref, wv_ref, wo_ref,
-                  w1_hbm, w3_hbm, w2_hbm, z_ref, f_ref, uall_ref, gall_ref,
-                  x_sc, acc_sc, u_sc, g_sc, sa, ra, sb, rb, sc, rc, sg, rg, ls, t1, t3, t2, q1, q3, q2s,
+                  w1_hbm, w3_hbm, w2_hbm, z_ref, f_ref, uall_ref, gall_ref, off_ref,
+                  x_sc, acc_sc, u_sc, g_sc, gv_sc, sa, ra, sb, rb, sc, rc, sg, rg, ls, lg, t1, t3, t2, q1, q3, q2s,
                   *, na_steps, nf_steps, hps, el, step_b, step_c):
     i = pl.program_id(0)
     t, d = h_ref.shape
@@ -207,10 +208,22 @@
             stage_b(n).wait_send()
         for n in range(3):
             stage_c(n).wait()
+        own()[0].wait()
+
+    @pl.when(i == na_steps + 1)
+    def _():
         for r in range(1, 8):
             stage_g(r).wait()
-        for c in own():
-            c.wait()
+        own()[1].wait()
+        back = pltpu.make_async_copy(gall_ref, gv_sc, lg.at[0])
+        back.start()
+        back.wait()
+        base = jnp.zeros((el, 1), jnp.int32)
+        for r in range(8):
+            off_ref[r] = jnp.broadcast_to(base, (el, 128))
+            cnt = jnp.sum(jnp.where(gv_sc[r] >= 0, 1.0, 0.0), axis=1, keepdims=True).astype(jnp.int32)
+            base = base + (cnt + 15) // 16 * 16
+        off_ref[8] = jnp.broadcast_to(jnp.maximum((base + MB - 1) // MB, 1), (el, 128))
 
 
 def _first(h, na, nm, nf, wr, idx, wq, wk, wv, wo, w1, w3, w2, el, nf_steps, ft):
@@ -238,12 +251,13 @@
         + [pl.BlockSpec((d, w), lambda i: (0, ai(i)))] * 3
         + [pl.BlockSpec((w, d), lambda i: (ai(i), 0))]
         + [any_] * 3,
-        out_specs=[full((t, d)), full((t, d)), any_, any_],
+        out_specs=[full((t, d)), full((t, d)), any_, any_, pl.BlockSpec((9, el, 128), lambda i: (0, 0, 0))],
         out_shape=[jax.ShapeDtypeStruct((t, d), BF), jax.ShapeDtypeStruct((t, d), F32),
-                   jax.ShapeDtypeStruct((8, t, d), BF), jax.ShapeDtypeStruct((8, el, t), F32)],
+                   jax.ShapeDtypeStruct((8, t, d), BF), jax.ShapeDtypeStruct((8, el, t), F32),
+                   jax.ShapeDtypeStruct((9, el, 128), jnp.int32)],
         scratch_shapes=[pltpu.VMEM((t, d), BF), pltpu.VMEM((t, d), F32), pltpu.VMEM((t, d), BF),
-                        pltpu.VMEM((ne, t), F32),
-                        dma((5,)), dma((5,)), dma((2,)), dma((2,)), dma((3,)), dma((3,)), dma((7,)), dma((7,)), dma((2,))] + _tile_scratch(d, ft),
+                        pltpu.VMEM((ne, t), F32), pltpu.VMEM((8, el, t), F32),
+                        dma((5,)), dma((5,)), dma((2,)), dma((2,)), dma((3,)), dma((3,)), dma((7,)), dma((7,)), dma((2,)), dma((1,))] + _tile_scratch(d, ft),
         cost_estimate=pl.CostEstimate(flops=8 * t * d * d, bytes_accessed=8 * d * d, transcendentals=0),
         compiler_params=pltpu.CompilerParams(dimension_semantics=("arbitrary",), collective_id=0, has_side_effects=True,
                                              vmem_limit_bytes=56 << 20),
@@ -251,7 +265,7 @@
     )(h, na, nm, nf, wr, idx, cos, sin, wq, wk, wv, wo, w1, w3, w2)
 
 
-def _hid_kernel(off_ref, nb_ref, g_ref, u_hbm, w1_hbm, w3_hbm, hid_hbm, gm_hbm,
+def _hid_kernel(off_ref, g_ref, u_hbm, w1_hbm, w3_hbm, hid_hbm, gm_hbm,
                 u_sc, x_sc, w1_sc, w3_sc, h_sc, hx_sc, gm_sc, su, sw1, sw3, sh, sg, *, ns, el, cap, nf, mb, depth):
     t, d = u_sc.shape[1:]
     ft = w1_sc.shape[-1]
@@ -310,7 +324,7 @@
             cs = slice(c * 512, (c + 1) * 512)
             xv = _dot(p, u_sc[s, :, cs]).astype(BF)
             for e in range(el):
-                o = pl.multiple_of(off_ref[s * el + e], 16)
+                o = pl.multiple_of(off_ref[s, e, 0], 16)
                 x_sc[e, pl.ds(o, cap), cs] = xv[e * cap:(e + 1) * cap]
 
     @pl.loop(0, total)
@@ -320,7 +334,7 @@
         for c in fetch(k):
             c.wait()
         for m in range(mb, rows + 1, mb):
-            @pl.when(nb_ref[e] == m // mb)
+            @pl.when(off_ref[ns, e, 0] == m // mb)
             def _():
                 x = x_sc[e, :m, :]
                 h1 = _dot(x, w1_sc[slot])
@@ -336,7 +350,7 @@
         def _():
             put_h(k - 2).wait()
         for s in range(ns):
-            o = pl.multiple_of(off_ref[s * el + e], 16)
+            o = pl.multiple_of(off_ref[s, e, 0], 16)
             hx_sc[lax.rem(k, 2), s * cap:(s + 1) * cap, :] = h_sc[pl.ds(o, cap), :]
         put_h(k).start()
 
@@ -346,20 +360,16 @@
         put_h(k).wait()
 
 
-def _hidden(u_all, g_all, ue1, ue3, cap):
+def _hidden(u_all, g_all, off, ue1, ue3, cap):
     ns, t, d = u_all.shape
     el, _, fe = ue1.shape
-    mb, nf, depth = 128, 2, 4
+    mb, nf, depth = MB, 2, 4
     ft = fe // nf
-    cnt = jnp.sum((g_all >= 0).astype(jnp.int32), axis=-1)
-    pad = (cnt + 15) // 16 * 16
-    off = jnp.cumsum(pad, axis=0) - pad
-    nb = jnp.maximum((jnp.sum(pad, axis=0) + mb - 1) // mb, 1)
     smem, vmem, any_ = (pl.BlockSpec(memory_space=m) for m in (pltpu.SMEM, pltpu.VMEM, pl.ANY))
     dma = pltpu.SemaphoreType.DMA
     return pl.pallas_call(
         functools.partial(_hid_kernel, ns=ns, el=el, cap=cap, nf=nf, mb=mb, depth=depth),
-        in_specs=[smem, smem, vmem, any_, any_, any_],
+        in_specs=[smem, vmem, any_, any_, any_],
         out_specs=[any_, any_],
         out_shape=[jax.ShapeDtypeStruct((el, ns * cap, fe), BF), jax.ShapeDtypeStruct((ns, t, 3 * el * cap), BF)],
         scratch_shapes=[pltpu.VMEM((ns, t, d), BF), pltpu.VMEM((el, ns * cap, d), BF), pltpu.VMEM((depth, d, ft), BF),
@@ -369,7 +379,7 @@
         cost_estimate=pl.CostEstimate(flops=4 * el * ns * cap * d * fe, bytes_accessed=4 * el * d * fe, transcendentals=0),
         compiler_params=pltpu.CompilerParams(vmem_limit_bytes=58 << 20),
         name="hidden",
-    )(off.reshape(-1), nb, g_all, u_all, ue1, ue3)
+    )(off, g_all, u_all, ue1, ue3)
 
 
 E0 = {q: q + 1 for q in range(8)}
@@ -420,8 +430,6 @@
         for c in get_zf():
             c.start()
         arrived()
-        for e in range(el):
-            get_h(e).wait()
 
     def pass_on(qs):
         for q in qs:
@@ -434,12 +442,21 @@
 
     pass_on((0, 1))
 
-    @pl.when(i < NQ)
+    def expert(e):
+        y = _dot(hid_sc[e], ue2_ref[e]).astype(BF)
+        for s in range(ns):
+            y_sc[s, e * cap:(e + 1) * cap, :] = y[s * cap:(s + 1) * cap]
+
+    @pl.when(i == 0)
     def _():
         for e in range(el):
-            y = _dot(hid_sc[e], ue2_ref[e]).astype(BF)
-            for s in range(ns):
-                y_sc[s, e * cap:(e + 1) * cap, :] = y[s * cap:(s + 1) * cap]
+            get_h(e).wait()
+            expert(e)
+
+    @pl.when((i > 0) & (i < NQ))
+    def _():
+        for e in range(el):
+            expert(e)
 
     pass_on(range(2, NQ))
 
@@ -457,8 +474,8 @@
     @pl.when(i < NQ)
     def _():
         kk = el * cap
-        for b in range(4):
-            for c in range(2):
+        for c in (1, 0):
+            for b in range(4):
                 s = 2 * b + c
                 y = y_sc[s]
                 m = _dot(gm_sc[s, :, :kk], y) + _dot(gm_sc[s, :, kk:2 * kk], y) + _dot(gm_sc[s, :, 2 * kk:], y)
@@ -468,7 +485,8 @@
                         keep_sc[h, pos] = part
                     else:
                         ps_sc[i % 2, h, pos] = part
-        send0(i, i % 2).start()
+            if c == 1:
+                send0(i, i % 2).start()
 
     @pl.when(i == F_FROM)
     def _():
@@ -545,9 +563,9 @@
         k = idx.shape[-1]
         el = ue1.shape[0]
         cap = 2 * t * k // (el * G)
-        z, f, u_all, g_all = _first(h0.reshape(t, d), na, nm, nf, wr.T, idx.reshape(t, k).T, wq, wk, wv, wo, w1, w3, w2,
+        z, f, u_all, g_all, off = _first(h0.reshape(t, d), na, nm, nf, wr.T, idx.reshape(t, k).T, wq, wk, wv, wo, w1, w3, w2,
                                     el, f0, ft)
-        hid, gm = _hidden(u_all, g_all, ue1, ue3, cap)
+        hid, gm = _hidden(u_all, g_all, off, ue1, ue3, cap)
         return _last(hid, gm, z, f, ue2, w1, w3, w2, cap, ft, f0).reshape(b, s, d)
 
     rows_spec = P(('dp', 'ep'))

time: 184 us -> 179 us (0.973)
  other arithmetic: 3.56 us -> 1.39 us
  Pallas kernels: 177 us -> 175 us
    pallas_call x1, Pallas kernels: 88 us -> 85.6 us  [_last(): pl.pallas_call(functools.partial(_last_kernel, ns=ns, el=el, cap=cap, f0=...]
where the time goes in v5:
time: 179 us
  Pallas kernels  175 us (98%)
  local copies, waits for them, and re-layouts  2.3 us (1%)
    pallas_call x1, Pallas kernels, _last(): pl.pallas_call(functools.partial(_last_kernel, ns=ns, el=el, cap=cap, f0=...  85.6 us
    pallas_call x1, Pallas kernels, _first(): pl.pallas_call(functools.partial(_first_kernel, na_steps=na_steps, nf_ste...  47.5 us
    pallas_call x1, Pallas kernels, _hidden(): pl.pallas_call(functools.partial(_hid_kernel, ns=ns, el=el, cap=cap, nf=n...  42.4 us

profile of v5, /device:TPU:0, one launch (start us, length us, event | category | flops | bytes accessed | tf_op | source)
XLA Modules:
  0.0 179.2 jit_solution(9826066189636918716)
XLA Ops:
  0.0 0.5 fusion
  0.6 0.8 pad_maximum_fusion
  1.4 47.5 %first.1 = (bf16[256,2048]{1,0:T(8,128)(2,1)}, f32[256,2048]{1,0:T(8,128)}, bf16[8,256,2048]{2,1,0:T(8,128)(2,1)}, f32[8,8,256]{2,1,0:T(8,128)}, s32[9,8,128]{2,1,0:T(8,128)}) custom-call(bf16[256,2048]{1,0:T(8,128)(2,1)} %bitcast.7, bf16[2048]{0:T(1024)(128)(2,1)} %na_ref.1, bf16[2048]{0:T(1024)(128)(2,1)} %nm_ref.1, bf16[2048]{0:T(1024)(128)(2,1)} %nf_ref.1, ...), custom_call_target="tpu_custom_call" | custom-call | flops 8589934592 | bytes 33554432 | tf_op jit(solution)/shard_map/first/pallas_call | solution.py:245
  48.9 42.4 %hidden.1 = (bf16[8,512,1024]{2,1,0:T(8,128)(2,1)}, bf16[8,256,1536]{2,1,0:T(8,128)(2,1)}) custom-call(s32[9,8,128]{2,1,0:T(8,128)} %get-tuple-element.12.off_ref, f32[8,8,256]{2,1,0:T(8,128)} %get-tuple-element.13.g_ref, bf16[8,256,2048]{2,1,0:T(8,128)(2,1)} %get-tuple-element.14.u_hbm, bf16[8,2048,1024]{2,1,0:T(8,128)(2,1)} %w1_hbm.4, ...), custom_call_target="tpu_custom_call" | custom-call | flops 34359738368 | bytes 67108864 | tf_op jit(solution)/shard_map/hidden/pallas_call | solution.py:370
  91.3 85.6 %last.1 = bf16[256,2048]{1,0:T(8,128)(2,1)} custom-call(bf16[8,512,1024]{2,1,0:T(8,128)(2,1)} %get-tuple-element.15.hid_hbm, bf16[8,256,1536]{2,1,0:T(8,128)(2,1)} %get-tuple-element.16.gm_hbm, bf16[256,2048]{1,0:T(8,128)(2,1)} %get-tuple-element.17.z_hbm, f32[256,2048]{1,0:T(8,128)} %get-tuple-element.18.f_hbm, bf16[8,1024,2048]{2,1,0:T(8,128)(2,1)} %ue2_ref.1, ...), custom_call_target="tpu_custom_call" | custom-call | flops 17179869184 | bytes 33554432 | tf_op jit(solution)/shard_map/last/pallas_call | solution.py:536
  176.9 2.3 %copy.18 = bf16[1,256,2048]{2,1,0:T(8,128)(2,1)} copy(bf16[1,256,2048]{2,1,0:T(8,128)(2,1)} %bitcast.6) | data formatting | bytes 2097152
  (2 shorter events, 0.0 us)

commit v6 on v5

--- a/solution.py
+++ b/solution.py
@@ -45,6 +45,12 @@
     return lambda: pl.semaphore_wait(sem, len(rels))
 
 
+def _rank(g):
+    t = g.shape[1]
+    before = jnp.where(lax.broadcasted_iota(jnp.int32, (t, t), 0) < lax.broadcasted_iota(jnp.int32, (t, t), 1), 1.0, 0.0)
+    return jnp.where(g >= 0, _dot(jnp.where(g >= 0, 1.0, 0.0), before), -1.0)
+
+
 class _Tiles:
     def __init__(self, hbm, vmem, sems, first, count):
         self.hbm, self.vmem, self.sems, self.first, self.count = hbm, vmem, sems, first, count
@@ -85,9 +91,9 @@
 
 
 def _first_kernel(h_ref, na_ref, nm_ref, nf_ref, wr_ref, idx_ref, cos_ref, sin_ref, wq_ref, wk_ref, wv_ref, wo_ref,
-                  w1_hbm, w3_hbm, w2_hbm, z_ref, f_ref, uall_ref, gall_ref, off_ref,
-                  x_sc, acc_sc, u_sc, g_sc, gv_sc, sa, ra, sb, rb, sc, rc, sg, rg, ls, lg, t1, t3, t2, q1, q3, q2s,
-                  *, na_steps, nf_steps, hps, el, step_b, step_c):
+                  w1_hbm, w3_hbm, w2_hbm, z_ref, f_ref, uall_ref, gall_ref, off_ref, gm_hbm,
+                  x_sc, acc_sc, u_sc, g_sc, gv_sc, gm_sc, sa, ra, sb, rb, sc, rc, sg, rg, ls, lg, t1, t3, t2, q1, q3, q2s,
+                  *, na_steps, nf_steps, hps, el, cap, step_b, step_c):
     i = pl.program_id(0)
     t, d = h_ref.shape
     me = lax.axis_index('ep')
@@ -108,7 +114,7 @@
 
     def stage_g(r):
         rows = pl.ds(pl.multiple_of(_peer(me, r) * el, el), el)
-        return remote(g_sc.at[rows], gall_ref.at[r], sg.at[r - 1], rg.at[r - 1], r)
+        return remote(g_sc.at[rows], gv_sc.at[r], sg.at[r - 1], rg.at[r - 1], r)
 
     def stage_b(n):
         rows = pl.ds(n * half, half)
@@ -118,9 +124,22 @@
         return remote(uall_ref.at[2 * n + 2], uall_ref.at[2 * n + 3], sc.at[n], rc.at[n], 1)
 
     def own():
-        rows = pl.ds(pl.multiple_of(me * el, el), el)
-        return (pltpu.make_async_copy(u_sc, uall_ref.at[0], ls.at[0]),
-                pltpu.make_async_copy(g_sc.at[rows], gall_ref.at[0], ls.at[1]))
+        return pltpu.make_async_copy(u_sc, uall_ref.at[0], ls.at[0])
+
+    def put_g(r):
+        return pltpu.make_async_copy(gm_sc.at[r % 2], gm_hbm.at[r], lg.at[r % 2])
+
+    def combine_matrix(r):
+        g = gv_sc[r]
+        it = lax.broadcasted_iota(jnp.int32, (cap, t), 0).astype(F32)
+        rank = _rank(g)
+        gt = jnp.concatenate([jnp.where(it == rank[e:e + 1, :], g[e:e + 1, :], 0.0) for e in range(el)], axis=0)
+        gm = jnp.transpose(gt)
+        ghi = gm.astype(BF)
+        r1 = gm - ghi.astype(F32)
+        gmid = r1.astype(BF)
+        glo = (r1 - gmid.astype(F32)).astype(BF)
+        gm_sc[r % 2] = jnp.concatenate([ghi, gmid, glo], axis=1)
 
     @pl.when(i == 0)
     def _():
@@ -140,10 +159,20 @@
             stage_a(n).start()
         for r in range(1, 8):
             stage_g(r).start()
-        for c in own():
-            c.start()
+        own().start()
+        gv_sc[0] = g_sc[pl.ds(pl.multiple_of(me * el, el), el), :]
         x_sc[...] = _rms(h_ref[...], na_ref[...])
         acc_sc[...] = jnp.zeros_like(acc_sc)
+
+    for r in range(8):
+        @pl.when(i == r + 1)
+        def _():
+            if r:
+                stage_g(r).wait_recv()
+            if r >= 2:
+                put_g(r - 2).wait()
+            combine_matrix(r)
+            put_g(r).start()
 
     @pl.when(i < na_steps)
     def _():
@@ -208,16 +237,15 @@
             stage_b(n).wait_send()
         for n in range(3):
             stage_c(n).wait()
-        own()[0].wait()
+        own().wait()
+        for r in (6, 7):
+            put_g(r).wait()
 
     @pl.when(i == na_steps + 1)
     def _():
         for r in range(1, 8):
-            stage_g(r).wait()
-        own()[1].wait()
-        back = pltpu.make_async_copy(gall_ref, gv_sc, lg.at[0])
-        back.start()
-        back.wait()
+            stage_g(r).wait_send()
+        gall_ref[...] = gv_sc[...]
         base = jnp.zeros((el, 1), jnp.int32)
         for r in range(8):
             off_ref[r] = jnp.broadcast_to(base, (el, 128))
@@ -226,7 +254,7 @@
         off_ref[8] = jnp.broadcast_to(jnp.maximum((base + MB - 1) // MB, 1), (el, 128))
 
 
-def _first(h, na, nm, nf, wr, idx, wq, wk, wv, wo, w1, w3, w2, el, nf_steps, ft):
+def _first(h, na, nm, nf, wr, idx, wq, wk, wv, wo, w1, w3, w2, el, cap, nf_steps, ft):
     t, d = h.shape
     hps = 2
     w = HEAD * hps
@@ -243,7 +271,7 @@
     any_ = pl.BlockSpec(memory_space=pl.ANY)
     dma = pltpu.SemaphoreType.DMA
     return pl.pallas_call(
-        functools.partial(_first_kernel, na_steps=na_steps, nf_steps=nf_steps, hps=hps, el=el, step_b=na_steps - 2,
+        functools.partial(_first_kernel, na_steps=na_steps, nf_steps=nf_steps, hps=hps, el=el, cap=cap, step_b=na_steps - 2,
                           step_c=na_steps + nf_steps),
         grid=(na_steps + nf_steps + 1,),
         in_specs=[full((t, d)), vec, vec, vec, full((ne, d)), full(idx.shape),
@@ -251,13 +279,14 @@
         + [pl.BlockSpec((d, w), lambda i: (0, ai(i)))] * 3
         + [pl.BlockSpec((w, d), lambda i: (ai(i), 0))]
         + [any_] * 3,
-        out_specs=[full((t, d)), full((t, d)), any_, any_, pl.BlockSpec((9, el, 128), lambda i: (0, 0, 0))],
+        out_specs=[full((t, d)), full((t, d)), any_, pl.BlockSpec((8, el, t), lambda i: (0, 0, 0)),
+                   pl.BlockSpec((9, el, 128), lambda i: (0, 0, 0)), any_],
         out_shape=[jax.ShapeDtypeStruct((t, d), BF), jax.ShapeDtypeStruct((t, d), F32),
                    jax.ShapeDtypeStruct((8, t, d), BF), jax.ShapeDtypeStruct((8, el, t), F32),
-                   jax.ShapeDtypeStruct((9, el, 128), jnp.int32)],
+                   jax.ShapeDtypeStruct((9, el, 128), jnp.int32), jax.ShapeDtypeStruct((8, t, 3 * el * cap), BF)],
         scratch_shapes=[pltpu.VMEM((t, d), BF), pltpu.VMEM((t, d), F32), pltpu.VMEM((t, d), BF),
-                        pltpu.VMEM((ne, t), F32), pltpu.VMEM((8, el, t), F32),
-                        dma((5,)), dma((5,)), dma((2,)), dma((2,)), dma((3,)), dma((3,)), dma((7,)), dma((7,)), dma((2,)), dma((1,))] + _tile_scratch(d, ft),
+                        pltpu.VMEM((ne, t), F32), pltpu.VMEM((8, el, t), F32), pltpu.VMEM((2, t, 3 * el * cap), BF),
+                        dma((5,)), dma((5,)), dma((2,)), dma((2,)), dma((3,)), dma((3,)), dma((7,)), dma((7,)), dma((1,)), dma((2,))] + _tile_scratch(d, ft),
         cost_estimate=pl.CostEstimate(flops=8 * t * d * d, bytes_accessed=8 * d * d, transcendentals=0),
         compiler_params=pltpu.CompilerParams(dimension_semantics=("arbitrary",), collective_id=0, has_side_effects=True,
                                              vmem_limit_bytes=56 << 20),
@@ -265,8 +294,8 @@
     )(h, na, nm, nf, wr, idx, cos, sin, wq, wk, wv, wo, w1, w3, w2)
 
 
-def _hid_kernel(off_ref, g_ref, u_hbm, w1_hbm, w3_hbm, hid_hbm, gm_hbm,
-                u_sc, x_sc, w1_sc, w3_sc, h_sc, hx_sc, gm_sc, su, sw1, sw3, sh, sg, *, ns, el, cap, nf, mb, depth):
+def _hid_kernel(off_ref, g_ref, u_hbm, w1_hbm, w3_hbm, hid_hbm,
+                u_sc, x_sc, w1_sc, w3_sc, h_sc, hx_sc, su, sw1, sw3, sh, *, ns, el, cap, nf, mb, depth):
     t, d = u_sc.shape[1:]
     ft = w1_sc.shape[-1]
     rows = ns * cap
@@ -284,10 +313,6 @@
         e, f = lax.div(k, nf), lax.rem(k, nf)
         cols = pl.ds(pl.multiple_of(f * ft, ft), ft)
         return pltpu.make_async_copy(hx_sc.at[slot], hid_hbm.at[e, :, cols], sh.at[slot])
-
-    def put_g(s):
-        slot = lax.rem(s, 2)
-        return pltpu.make_async_copy(gm_sc.at[slot], gm_hbm.at[s], sg.at[slot])
 
     def get_u(s):
         return pltpu.make_async_copy(u_hbm.at[s], u_sc.at[s], su.at[s])
@@ -299,26 +324,11 @@
             c.start()
     h_sc[...] = jnp.zeros_like(h_sc)
     it = lax.broadcasted_iota(jnp.int32, (cap, t), 0).astype(F32)
-    before = jnp.where(lax.broadcasted_iota(jnp.int32, (t, t), 0) < lax.broadcasted_iota(jnp.int32, (t, t), 1), 1.0, 0.0)
 
     @pl.loop(0, ns)
     def _(s):
-        g = g_ref[s]
-        rank = jnp.where(g >= 0, _dot(jnp.where(g >= 0, 1.0, 0.0), before), -1.0)
-        hit = [it == rank[e:e + 1, :] for e in range(el)]
-        p = jnp.concatenate([jnp.where(h, 1.0, 0.0).astype(BF) for h in hit], axis=0)
-        gt = jnp.concatenate([jnp.where(h, g[e:e + 1, :], 0.0) for e, h in enumerate(hit)], axis=0)
-        gm = jnp.transpose(gt)
-        ghi = gm.astype(BF)
-        r1 = gm - ghi.astype(F32)
-        gmid = r1.astype(BF)
-        glo = (r1 - gmid.astype(F32)).astype(BF)
-
-        @pl.when(s >= 2)
-        def _():
-            put_g(s - 2).wait()
-        gm_sc[lax.rem(s, 2)] = jnp.concatenate([ghi, gmid, glo], axis=1)
-        put_g(s).start()
+        rank = _rank(g_ref[s])
+        p = jnp.concatenate([jnp.where(it == rank[e:e + 1, :], 1.0, 0.0).astype(BF) for e in range(el)], axis=0)
         get_u(s).wait()
         for c in range(d // 512):
             cs = slice(c * 512, (c + 1) * 512)
@@ -354,8 +364,6 @@
             hx_sc[lax.rem(k, 2), s * cap:(s + 1) * cap, :] = h_sc[pl.ds(o, cap), :]
         put_h(k).start()
 
-    for s in (ns - 2, ns - 1):
-        put_g(s).wait()
     for k in (total - 2, total - 1):
         put_h(k).wait()
 
@@ -370,12 +378,11 @@
     return pl.pallas_call(
         functools.partial(_hid_kernel, ns=ns, el=el, cap=cap, nf=nf, mb=mb, depth=depth),
         in_specs=[smem, vmem, any_, any_, any_],
-        out_specs=[any_, any_],
-        out_shape=[jax.ShapeDtypeStruct((el, ns * cap, fe), BF), jax.ShapeDtypeStruct((ns, t, 3 * el * cap), BF)],
+        out_specs=any_,
+        out_shape=jax.ShapeDtypeStruct((el, ns * cap, fe), BF),
         scratch_shapes=[pltpu.VMEM((ns, t, d), BF), pltpu.VMEM((el, ns * cap, d), BF), pltpu.VMEM((depth, d, ft), BF),
                         pltpu.VMEM((depth, d, ft), BF), pltpu.VMEM((ns * cap, ft), BF), pltpu.VMEM((2, ns * cap, ft), BF),
-                        pltpu.VMEM((2, t, 3 * el * cap), BF),
-                        dma((ns,)), dma((depth,)), dma((depth,)), dma((2,)), dma((2,))],
+                        dma((ns,)), dma((depth,)), dma((depth,)), dma((2,))],
         cost_estimate=pl.CostEstimate(flops=4 * el * ns * cap * d * fe, bytes_accessed=4 * el * d * fe, transcendentals=0),
         compiler_params=pltpu.CompilerParams(vmem_limit_bytes=58 << 20),
         name="hidden",
@@ -563,9 +570,9 @@
         k = idx.shape[-1]
         el = ue1.shape[0]
         cap = 2 * t * k // (el * G)
-        z, f, u_all, g_all, off = _first(h0.reshape(t, d), na, nm, nf, wr.T, idx.reshape(t, k).T, wq, wk, wv, wo, w1, w3, w2,
-                                    el, f0, ft)
-        hid, gm = _hidden(u_all, g_all, off, ue1, ue3, cap)
+        z, f, u_all, g_all, off, gm = _first(h0.reshape(t, d), na, nm, nf, wr.T, idx.reshape(t, k).T, wq, wk, wv, wo, w1, w3, w2,
+                                         el, cap, f0, ft)
+        hid = _hidden(u_all, g_all, off, ue1, ue3, cap)
         return _last(hid, gm, z, f, ue2, w1, w3, w2, cap, ft, f0).reshape(b, s, d)
 
     rows_spec = P(('dp', 'ep'))

time: 179 us -> 193 us (1.078)
  Pallas kernels: 175 us -> 190 us
    pallas_call x1, Pallas kernels: 47.5 us -> 63.6 us  [_first(): pl.pallas_call(functools.partial(_first_kernel, na_steps=na_steps, nf_ste...]
    pallas_call x1, Pallas kernels: 42.4 us -> 40.4 us  [_hidden(): pl.pallas_call(functools.partial(_hid_kernel, ns=ns, el=el, cap=cap, nf=n...]
where the time goes in v6:
time: 193 us
  Pallas kernels  190 us (98%)
  local copies, waits for them, and re-layouts  2.3 us (1%)
    pallas_call x1, Pallas kernels, _last(): pl.pallas_call(functools.partial(_last_kernel, ns=ns, el=el, cap=cap, f0=...  85.6 us
    pallas_call x1, Pallas kernels, _first(): pl.pallas_call(functools.partial(_first_kernel, na_steps=na_steps, nf_ste...  63.6 us
    pallas_call x1, Pallas kernels, _hidden(): pl.pallas_call(functools.partial(_hid_kernel, ns=ns, el=el, cap=cap, nf=n...  40.4 us

profile of v6, /device:TPU:0, one launch (start us, length us, event | category | flops | bytes accessed | tf_op | source)
XLA Modules:
  0.0 193.3 jit_solution(7255080029921835226)
XLA Ops:
  0.0 0.5 fusion
  0.6 0.9 pad_maximum_fusion
  1.4 63.6 %first.1 = (bf16[256,2048]{1,0:T(8,128)(2,1)}, f32[256,2048]{1,0:T(8,128)}, bf16[8,256,2048]{2,1,0:T(8,128)(2,1)}, f32[8,8,256]{2,1,0:T(8,128)}, s32[9,8,128]{2,1,0:T(8,128)}, /*index=5*/bf16[8,256,1536]{2,1,0:T(8,128)(2,1)}) custom-call(bf16[256,2048]{1,0:T(8,128)(2,1)} %bitcast.7, bf16[2048]{0:T(1024)(128)(2,1)} %na_ref.1, bf16[2048]{0:T(1024)(128)(2,1)} %nm_ref.1, ...), custom_call_target="tpu_custom_call" | custom-call | flops 8589934592 | bytes 33554432 | tf_op jit(solution)/shard_map/first/pallas_call | solution.py:273
  65.0 40.4 %hidden.1.hid_hbm = bf16[8,512,1024]{2,1,0:T(8,128)(2,1)} custom-call(s32[9,8,128]{2,1,0:T(8,128)} %get-tuple-element.11.off_ref, f32[8,8,256]{2,1,0:T(8,128)} %get-tuple-element.12.g_ref, bf16[8,256,2048]{2,1,0:T(8,128)(2,1)} %get-tuple-element.13.u_hbm, bf16[8,2048,1024]{2,1,0:T(8,128)(2,1)} %w1_hbm.4, bf16[8,2048,1024]{2,1,0:T(8,128)(2,1)} %w3_hbm.4), custom_call_target="tpu_custom_call" | custom-call | flops 34359738368 | bytes 67108864 | tf_op jit(solution)/shard_map/hidden/pallas_call | solution.py:378
  105.4 85.6 %last.1 = bf16[256,2048]{1,0:T(8,128)(2,1)} custom-call(bf16[8,512,1024]{2,1,0:T(8,128)(2,1)} %hidden.1.hid_hbm, bf16[8,256,1536]{2,1,0:T(8,128)(2,1)} %get-tuple-element.14.gm_hbm, bf16[256,2048]{1,0:T(8,128)(2,1)} %get-tuple-element.15.z_hbm, f32[256,2048]{1,0:T(8,128)} %get-tuple-element.16.f_hbm, bf16[8,1024,2048]{2,1,0:T(8,128)(2,1)} %ue2_ref.1, ...), custom_call_target="tpu_custom_call" | custom-call | flops 17179869184 | bytes 33554432 | tf_op jit(solution)/shard_map/last/pallas_call | solution.py:543
  191.0 2.3 %copy.18 = bf16[1,256,2048]{2,1,0:T(8,128)(2,1)} copy(bf16[1,256,2048]{2,1,0:T(8,128)(2,1)} %bitcast.6) | data formatting | bytes 2097152
  (2 shorter events, 0.0 us)
